TPU v7x, 32 devices: a whole 2x2x4 slice. The times are simulated.
32 devices in a mesh: group: 2 (over y), member: 16 (over z, x, core).
Axes of the slice: x: 2, y: 2, z: 4, core: 2. Of those that a mesh axis runs over, the one named last changes fastest.
Arguments:
- state: float32 [512, 64, 128], P(('group', 'member')), may hold values from -2.5 to 2.5
- blocks: bfloat16 [512, 6, 128, 128], P(('group', 'member')), may hold values from -1 to 1
- rate: float32 [512, 128], P(('group', 'member')), may hold values from 0.1 to 1
- own_col: int32 [512], P(('group', 'member')), may hold values from 0 to 15
- member_col: int32 [512, 4], P(('group', 'member')), may hold values from 0 to 15, as said below
- group_col: int32 [512, 1], P(('group', 'member')), may hold values from 0 to 3, as said below
- member_send: int32 [32, 16], P(('group', 'member')), may hold values from 0 to 15
- group_send: int32 [32, 4], P(('group', 'member')), may hold values from 0 to 15
Outputs:
- new_state: float32 [512, 64, 128], P(('group', 'member'))
Inputs may be any that keep to these rules, and one draw needn't show every extreme that they name: `member_col`: on each device the 64 entries of its rows name every member index equally often. `group_col`: on each device the 16 entries of its rows name every slot equally often.
All inputs are finite; a program needn't handle non-finite values.
Results may differ from a plain program's by a relative error of at most 0.00092.
Values may be sent and summed in bfloat16 or wider, within the bound.
No kernel may reach another device: no remote copies, remote signals or barrier semaphores. Data moves between devices by JAX's collectives and lax.ppermute only.
A program may use at most 64 MiB of HBM per device.

v0:
```python
import jax
import jax.numpy as jnp
from jax import lax
from jax.sharding import PartitionSpec as P

STEPS = 2


step_size = 0.1


def per_device(state, blocks, rate, own_col, member_col, group_col, member_send, group_send):
    members = member_col.shape[1]

    def derivative(field):
        rounded = field.astype(jnp.bfloat16)
        member_out = rounded[member_send[0]]
        group_out = rounded[group_send[0]]
        far_blocks = lax.all_to_all(group_out, "group", split_axis=0, concat_axis=0, tiled=True)
        own_rows = rounded[own_col]
        far_rows = far_blocks[group_col]
        own_term = jnp.einsum(
            "itc,icd->itd", own_rows, blocks[:, 0], preferred_element_type=jnp.float32
        )
        far_term = jnp.einsum(
            "iktc,ikcd->itd", far_rows, blocks[:, 1 + members :], preferred_element_type=jnp.float32
        )
        taken = lax.all_to_all(member_out, "member", split_axis=0, concat_axis=0, tiled=True)[
            member_col
        ]
        near_term = jnp.einsum(
            "iktc,ikcd->itd", taken, blocks[:, 1 : 1 + members], preferred_element_type=jnp.float32
        )
        product = own_term + far_term + near_term
        return -product + rate[:, None, :] * (field - field * field * field)

    current = state
    for step in range(STEPS):
        first = derivative(current)
        second = derivative(current + 0.5 * step_size * first)
        third = derivative(current + 0.5 * step_size * second)
        fourth = derivative(current + step_size * third)
        current = current + step_size / 6.0 * (first + 2.0 * second + 2.0 * third + fourth)
    return current


def solution(mesh):
    return jax.shard_map(
        per_device,
        mesh=mesh,
        in_specs=(
            P(("group", "member"), None, None),
            P(("group", "member"), None, None, None),
            P(("group", "member"), None),
            P(("group", "member")),
            P(("group", "member"), None),
            P(("group", "member"), None),
            P(("group", "member"), None),
            P(("group", "member"), None),
        ),
        out_specs=P(("group", "member"), None, None),
        check_vma=False,
    )
```

profile of v0, /device:TPU:0, one launch (start us, length us, event | category | flops | bytes accessed | tf_op | source)
XLA Modules:
  0.0 222.1 jit_solution(13842656189816934914)
XLA Ops:
  3.2 4.3 %all-to-all-start = ((bf16[4,64,128]{2,1,0:T(8,128)(2,1)}), bf16[4,64,128]{2,1,0:T(8,128)(2,1)S(1)}, u32[]{:S(2)}, u32[]{:S(2)}) async-start(bf16[4,64,128]{2,1,0:T(8,128)(2,1)} %gather_fusion.1), calls=%async_computation | async-start | bytes 131072 | tf_op jit(solution)/shard_map/all_to_all | solution.py:19
  12.9 6.6 %all-to-all-start.1 = ((bf16[16,64,128]{2,1,0:T(8,128)(2,1)}), bf16[16,64,128]{2,1,0:T(8,128)(2,1)S(1)}, u32[]{:S(2)}, u32[]{:S(2)}) async-start(bf16[16,64,128]{2,1,0:T(8,128)(2,1)} %gather_fusion.3), calls=%async_computation.1 | async-start | bytes 524288 | tf_op jit(solution)/shard_map/all_to_all | solution.py:28
  19.5 2.2 fusion.60
  23.0 2.2 convolution_add_fusion.7
  25.2 4.3 %all-to-all-done.1 = bf16[16,64,128]{2,1,0:T(8,128)(2,1)S(1)} async-done(((bf16[16,64,128]{2,1,0:T(8,128)(2,1)}), bf16[16,64,128]{2,1,0:T(8,128)(2,1)S(1)}, u32[]{:S(2)}, u32[]{:S(2)}) %all-to-all-start.1) | async-done | bytes 262176 | tf_op jit(solution)/shard_map/all_to_all | solution.py:28
  31.2 2.9 %fusion.72 = (bf16[16,64,128]{2,1,0:T(8,128)(2,1)S(1)}, f32[16,64,128]{2,1,0:T(8,128)}) fusion(f32[16,64,128]{2,1,0:T(8,128)} %param.8, f32[16,128]{1,0:T(8,128)S(1)} %copy-done.1, f32[16,64,128]{2,1,0:T(8,128)} %convolution_add_fusion.7, bf16[16,4,64,128]{3,2,1,0:T(8,128)(2,1)} %bitcast.166, bf16[16,6,128,128]{3,2,1,0:T(8,128)(2,1)S(1)} %copy-done), kind=kOutput, calls=%fused_computation.142 | convolution fusion | flops 135528448 | bytes 4988928 | tf_op jit(solution)/shard_map/iktc,ikcd->itd/dot_general | solution.py:31
  35.2 3.3 %all-to-all-start.2 = ((bf16[4,64,128]{2,1,0:T(8,128)(2,1)}), bf16[4,64,128]{2,1,0:T(8,128)(2,1)S(1)}, u32[]{:S(2)}, u32[]{:S(2)}) async-start(bf16[4,64,128]{2,1,0:T(8,128)(2,1)} %gather_fusion.6), calls=%async_computation.2 | async-start | bytes 131072 | tf_op jit(solution)/shard_map/all_to_all | solution.py:19
  42.6 3.5 %all-to-all-start.3 = ((bf16[16,64,128]{2,1,0:T(8,128)(2,1)}), bf16[16,64,128]{2,1,0:T(8,128)(2,1)S(1)}, u32[]{:S(2)}, u32[]{:S(2)}) async-start(bf16[16,64,128]{2,1,0:T(8,128)(2,1)} %gather_fusion.8), calls=%async_computation.3 | async-start | bytes 524288 | tf_op jit(solution)/shard_map/all_to_all | solution.py:28
  46.2 2.0 fusion.58
  49.5 2.2 convolution_add_fusion.6
  51.7 4.5 %all-to-all-done.3 = bf16[16,64,128]{2,1,0:T(8,128)(2,1)S(1)} async-done(((bf16[16,64,128]{2,1,0:T(8,128)(2,1)}), bf16[16,64,128]{2,1,0:T(8,128)(2,1)S(1)}, u32[]{:S(2)}, u32[]{:S(2)}) %all-to-all-start.3) | async-done | bytes 262176 | tf_op jit(solution)/shard_map/all_to_all | solution.py:28
  57.8 3.0 %fusion.73 = (bf16[16,64,128]{2,1,0:T(8,128)(2,1)S(1)}, f32[16,64,128]{2,1,0:T(8,128)}) fusion(f32[16,64,128]{2,1,0:T(8,128)} %param.8, f32[16,64,128]{2,1,0:T(8,128)} %get-tuple-element.6, f32[16,128]{1,0:T(8,128)S(1)} %copy-done.1, f32[16,64,128]{2,1,0:T(8,128)} %convolution_add_fusion.6, bf16[16,4,64,128]{3,2,1,0:T(8,128)(2,1)} %bitcast.168, ...), kind=kOutput, calls=%fused_computation.143 | convolution fusion | flops 135790592 | bytes 5513216 | tf_op jit(solution)/shard_map/iktc,ikcd->itd/dot_general | solution.py:31
  62.0 3.3 %all-to-all-start.4 = ((bf16[4,64,128]{2,1,0:T(8,128)(2,1)}), bf16[4,64,128]{2,1,0:T(8,128)(2,1)S(1)}, u32[]{:S(2)}, u32[]{:S(2)}) async-start(bf16[4,64,128]{2,1,0:T(8,128)(2,1)} %gather_fusion.11), calls=%async_computation.4 | async-start | bytes 131072 | tf_op jit(solution)/shard_map/all_to_all | solution.py:19
  69.4 3.5 %all-to-all-start.5 = ((bf16[16,64,128]{2,1,0:T(8,128)(2,1)}), bf16[16,64,128]{2,1,0:T(8,128)(2,1)S(1)}, u32[]{:S(2)}, u32[]{:S(2)}) async-start(bf16[16,64,128]{2,1,0:T(8,128)(2,1)} %gather_fusion.13), calls=%async_computation.5 | async-start | bytes 524288 | tf_op jit(solution)/shard_map/all_to_all | solution.py:28
  72.9 2.0 fusion.56
  76.3 2.2 convolution_add_fusion.5
  78.5 4.5 %all-to-all-done.5 = bf16[16,64,128]{2,1,0:T(8,128)(2,1)S(1)} async-done(((bf16[16,64,128]{2,1,0:T(8,128)(2,1)}), bf16[16,64,128]{2,1,0:T(8,128)(2,1)S(1)}, u32[]{:S(2)}, u32[]{:S(2)}) %all-to-all-start.5) | async-done | bytes 262176 | tf_op jit(solution)/shard_map/all_to_all | solution.py:28
  84.6 3.0 %fusion.62 = (bf16[16,64,128]{2,1,0:T(8,128)(2,1)S(1)}, f32[16,64,128]{2,1,0:T(8,128)}) fusion(f32[16,64,128]{2,1,0:T(8,128)} %param.8, f32[16,64,128]{2,1,0:T(8,128)} %get-tuple-element.8, f32[16,128]{1,0:T(8,128)S(1)} %copy-done.1, f32[16,64,128]{2,1,0:T(8,128)} %convolution_add_fusion.5, bf16[16,4,64,128]{3,2,1,0:T(8,128)(2,1)} %bitcast.169, ...), kind=kOutput, calls=%fused_computation.132 | convolution fusion | flops 135790592 | bytes 5513216 | tf_op jit(solution)/shard_map/iktc,ikcd->itd/dot_general | solution.py:31
  88.8 3.3 %all-to-all-start.6 = ((bf16[4,64,128]{2,1,0:T(8,128)(2,1)}), bf16[4,64,128]{2,1,0:T(8,128)(2,1)S(1)}, u32[]{:S(2)}, u32[]{:S(2)}) async-start(bf16[4,64,128]{2,1,0:T(8,128)(2,1)} %gather_fusion.16), calls=%async_computation.6 | async-start | bytes 131072 | tf_op jit(solution)/shard_map/all_to_all | solution.py:19
  96.2 3.5 %all-to-all-start.7 = ((bf16[16,64,128]{2,1,0:T(8,128)(2,1)}), bf16[16,64,128]{2,1,0:T(8,128)(2,1)S(1)}, u32[]{:S(2)}, u32[]{:S(2)}) async-start(bf16[16,64,128]{2,1,0:T(8,128)(2,1)} %gather_fusion.18), calls=%async_computation.7 | async-start | bytes 524288 | tf_op jit(solution)/shard_map/all_to_all | solution.py:28
  99.7 2.0 fusion.54
  103.0 2.2 convolution_add_fusion.4
  105.2 4.5 %all-to-all-done.7 = bf16[16,64,128]{2,1,0:T(8,128)(2,1)S(1)} async-done(((bf16[16,64,128]{2,1,0:T(8,128)(2,1)}), bf16[16,64,128]{2,1,0:T(8,128)(2,1)S(1)}, u32[]{:S(2)}, u32[]{:S(2)}) %all-to-all-start.7) | async-done | bytes 262176 | tf_op jit(solution)/shard_map/all_to_all | solution.py:28
  111.4 3.4 %fusion.95 = (bf16[16,64,128]{2,1,0:T(8,128)(2,1)S(1)}, f32[16,64,128]{2,1,0:T(8,128)}) fusion(f32[16,64,128]{2,1,0:T(8,128)} %param.8, f32[16,64,128]{2,1,0:T(8,128)} %get-tuple-element.10, f32[16,128]{1,0:T(8,128)S(1)} %copy-done.1, f32[16,64,128]{2,1,0:T(8,128)} %convolution_add_fusion.4, bf16[16,4,64,128]{3,2,1,0:T(8,128)(2,1)} %bitcast.164, ...), kind=kOutput, calls=%fused_computation.175 | convolution fusion | flops 136445952 | bytes 6561792 | tf_op jit(solution)/shard_map/iktc,ikcd->itd/dot_general | solution.py:31
  115.9 3.3 %all-to-all-start.8 = ((bf16[4,64,128]{2,1,0:T(8,128)(2,1)}), bf16[4,64,128]{2,1,0:T(8,128)(2,1)S(1)}, u32[]{:S(2)}, u32[]{:S(2)}) async-start(bf16[4,64,128]{2,1,0:T(8,128)(2,1)} %gather_fusion.21), calls=%async_computation.8 | async-start | bytes 131072 | tf_op jit(solution)/shard_map/all_to_all | solution.py:19
  123.3 3.5 %all-to-all-start.9 = ((bf16[16,64,128]{2,1,0:T(8,128)(2,1)}), bf16[16,64,128]{2,1,0:T(8,128)(2,1)S(1)}, u32[]{:S(2)}, u32[]{:S(2)}) async-start(bf16[16,64,128]{2,1,0:T(8,128)(2,1)} %gather_fusion.23), calls=%async_computation.9 | async-start | bytes 524288 | tf_op jit(solution)/shard_map/all_to_all | solution.py:28
  126.9 2.0 fusion.52
  130.2 2.2 convolution_add_fusion.3
  132.4 4.5 %all-to-all-done.9 = bf16[16,64,128]{2,1,0:T(8,128)(2,1)S(1)} async-done(((bf16[16,64,128]{2,1,0:T(8,128)(2,1)}), bf16[16,64,128]{2,1,0:T(8,128)(2,1)S(1)}, u32[]{:S(2)}, u32[]{:S(2)}) %all-to-all-start.9) | async-done | bytes 262176 | tf_op jit(solution)/shard_map/all_to_all | solution.py:28
  138.5 2.9 %fusion.74 = (bf16[16,64,128]{2,1,0:T(8,128)(2,1)S(1)}, f32[16,64,128]{2,1,0:T(8,128)}) fusion(f32[16,64,128]{2,1,0:T(8,128)} %get-tuple-element.12, f32[16,128]{1,0:T(8,128)S(1)} %copy-done.1, f32[16,64,128]{2,1,0:T(8,128)} %convolution_add_fusion.3, bf16[16,4,64,128]{3,2,1,0:T(8,128)(2,1)} %bitcast.165, bf16[16,6,128,128]{3,2,1,0:T(8,128)(2,1)S(1)} %copy-done), kind=kOutput, calls=%fused_computation.144 | convolution fusion | flops 135528448 | bytes 4988928 | tf_op jit(solution)/shard_map/iktc,ikcd->itd/dot_general | solution.py:31
  142.5 3.3 %all-to-all-start.10 = ((bf16[4,64,128]{2,1,0:T(8,128)(2,1)}), bf16[4,64,128]{2,1,0:T(8,128)(2,1)S(1)}, u32[]{:S(2)}, u32[]{:S(2)}) async-start(bf16[4,64,128]{2,1,0:T(8,128)(2,1)} %gather_fusion.26), calls=%async_computation.10 | async-start | bytes 131072 | tf_op jit(solution)/shard_map/all_to_all | solution.py:19
  150.0 3.5 %all-to-all-start.11 = ((bf16[16,64,128]{2,1,0:T(8,128)(2,1)}), bf16[16,64,128]{2,1,0:T(8,128)(2,1)S(1)}, u32[]{:S(2)}, u32[]{:S(2)}) async-start(bf16[16,64,128]{2,1,0:T(8,128)(2,1)} %gather_fusion.28), calls=%async_computation.11 | async-start | bytes 524288 | tf_op jit(solution)/shard_map/all_to_all | solution.py:28
  153.5 2.0 fusion.50
  156.8 2.2 convolution_add_fusion.2
  159.0 4.5 %all-to-all-done.11 = bf16[16,64,128]{2,1,0:T(8,128)(2,1)S(1)} async-done(((bf16[16,64,128]{2,1,0:T(8,128)(2,1)}), bf16[16,64,128]{2,1,0:T(8,128)(2,1)S(1)}, u32[]{:S(2)}, u32[]{:S(2)}) %all-to-all-start.11) | async-done | bytes 262176 | tf_op jit(solution)/shard_map/all_to_all | solution.py:28
  165.1 3.0 %fusion.75 = (bf16[16,64,128]{2,1,0:T(8,128)(2,1)S(1)}, f32[16,64,128]{2,1,0:T(8,128)}) fusion(f32[16,64,128]{2,1,0:T(8,128)} %get-tuple-element.12, f32[16,64,128]{2,1,0:T(8,128)} %get-tuple-element.14, f32[16,128]{1,0:T(8,128)S(1)} %copy-done.1, f32[16,64,128]{2,1,0:T(8,128)} %convolution_add_fusion.2, bf16[16,4,64,128]{3,2,1,0:T(8,128)(2,1)} %bitcast.170, ...), kind=kOutput, calls=%fused_computation.145 | convolution fusion | flops 135790592 | bytes 5513216 | tf_op jit(solution)/shard_map/iktc,ikcd->itd/dot_general | solution.py:31
  169.3 3.3 %all-to-all-start.12 = ((bf16[4,64,128]{2,1,0:T(8,128)(2,1)}), bf16[4,64,128]{2,1,0:T(8,128)(2,1)S(1)}, u32[]{:S(2)}, u32[]{:S(2)}) async-start(bf16[4,64,128]{2,1,0:T(8,128)(2,1)} %gather_fusion.31), calls=%async_computation.12 | async-start | bytes 131072 | tf_op jit(solution)/shard_map/all_to_all | solution.py:19
  176.7 3.5 %all-to-all-start.13 = ((bf16[16,64,128]{2,1,0:T(8,128)(2,1)}), bf16[16,64,128]{2,1,0:T(8,128)(2,1)S(1)}, u32[]{:S(2)}, u32[]{:S(2)}) async-start(bf16[16,64,128]{2,1,0:T(8,128)(2,1)} %gather_fusion.33), calls=%async_computation.13 | async-start | bytes 524288 | tf_op jit(solution)/shard_map/all_to_all | solution.py:28
  180.3 2.0 fusion.48
  183.6 2.2 convolution_add_fusion.1
  185.8 4.5 %all-to-all-done.13 = bf16[16,64,128]{2,1,0:T(8,128)(2,1)S(1)} async-done(((bf16[16,64,128]{2,1,0:T(8,128)(2,1)}), bf16[16,64,128]{2,1,0:T(8,128)(2,1)S(1)}, u32[]{:S(2)}, u32[]{:S(2)}) %all-to-all-start.13) | async-done | bytes 262176 | tf_op jit(solution)/shard_map/all_to_all | solution.py:28
  191.9 3.0 %fusion.63 = (bf16[16,64,128]{2,1,0:T(8,128)(2,1)S(1)}, f32[16,64,128]{2,1,0:T(8,128)}) fusion(f32[16,64,128]{2,1,0:T(8,128)} %get-tuple-element.12, f32[16,64,128]{2,1,0:T(8,128)} %get-tuple-element.16, f32[16,128]{1,0:T(8,128)S(1)} %copy-done.1, f32[16,64,128]{2,1,0:T(8,128)} %convolution_add_fusion.1, bf16[16,4,64,128]{3,2,1,0:T(8,128)(2,1)} %bitcast.171, ...), kind=kOutput, calls=%fused_computation.133 | convolution fusion | flops 135790592 | bytes 5513216 | tf_op jit(solution)/shard_map/iktc,ikcd->itd/dot_general | solution.py:31
  196.1 3.3 %all-to-all-start.14 = ((bf16[4,64,128]{2,1,0:T(8,128)(2,1)}), bf16[4,64,128]{2,1,0:T(8,128)(2,1)S(1)}, u32[]{:S(2)}, u32[]{:S(2)}) async-start(bf16[4,64,128]{2,1,0:T(8,128)(2,1)} %gather_fusion.36), calls=%async_computation.14 | async-start | bytes 131072 | tf_op jit(solution)/shard_map/all_to_all | solution.py:19
  203.5 3.5 %all-to-all-start.15 = ((bf16[16,64,128]{2,1,0:T(8,128)(2,1)}), bf16[16,64,128]{2,1,0:T(8,128)(2,1)S(1)}, u32[]{:S(2)}, u32[]{:S(2)}) async-start(bf16[16,64,128]{2,1,0:T(8,128)(2,1)} %gather_fusion.38), calls=%async_computation.15 | async-start | bytes 524288 | tf_op jit(solution)/shard_map/all_to_all | solution.py:28
  207.1 2.0 fusion.46
  210.4 2.2 convolution_add_fusion
  212.6 4.5 %all-to-all-done.15 = bf16[16,64,128]{2,1,0:T(8,128)(2,1)S(1)} async-done(((bf16[16,64,128]{2,1,0:T(8,128)(2,1)}), bf16[16,64,128]{2,1,0:T(8,128)(2,1)S(1)}, u32[]{:S(2)}, u32[]{:S(2)}) %all-to-all-start.15) | async-done | bytes 262176 | tf_op jit(solution)/shard_map/all_to_all | solution.py:28
  218.7 3.4 %fusion.29 = f32[16,64,128]{2,1,0:T(8,128)} fusion(f32[16,64,128]{2,1,0:T(8,128)} %get-tuple-element.12, f32[16,64,128]{2,1,0:T(8,128)} %convolution_add_fusion, bf16[16,4,64,128]{3,2,1,0:T(8,128)(2,1)} %bitcast.167, f32[16,64,128]{2,1,0:T(8,128)} %get-tuple-element.18, f32[16,64,128]{2,1,0:T(8,128)} %get-tuple-element.14, ...), kind=kOutput, calls=%fused_computation.77 | convolution fusion | flops 136314880 | bytes 6299648 | tf_op jit(solution)/shard_map/iktc,ikcd->itd/dot_general | solution.py:31
  (65 shorter events, 69.1 us)
Async XLA Ops:
  0.0 23.0 %copy-start = (bf16[16,6,128,128]{3,2,1,0:T(8,128)(2,1)S(1)}, bf16[16,6,128,128]{3,2,1,0:T(8,128)(2,1)}, u32[]{:S(2)}) copy-start(bf16[16,6,128,128]{3,2,1,0:T(8,128)(2,1)} %param.9) | copy-start | bytes 9437188
  3.2 9.7 %all-to-all-start = ((bf16[4,64,128]{2,1,0:T(8,128)(2,1)}), bf16[4,64,128]{2,1,0:T(8,128)(2,1)S(1)}, u32[]{:S(2)}, u32[]{:S(2)}) async-start(bf16[4,64,128]{2,1,0:T(8,128)(2,1)} %gather_fusion.1), calls=%async_computation | async-start | bytes 131072 | tf_op jit(solution)/shard_map/all_to_all | solution.py:19
  12.9 18.2 %copy-start.1 = (f32[16,128]{1,0:T(8,128)S(1)}, f32[16,128]{1,0:T(8,128)}, u32[]{:S(2)}) copy-start(f32[16,128]{1,0:T(8,128)} %param.10) | copy-start | bytes 24580
  12.9 16.6 %all-to-all-start.1 = ((bf16[16,64,128]{2,1,0:T(8,128)(2,1)}), bf16[16,64,128]{2,1,0:T(8,128)(2,1)S(1)}, u32[]{:S(2)}, u32[]{:S(2)}) async-start(bf16[16,64,128]{2,1,0:T(8,128)(2,1)} %gather_fusion.3), calls=%async_computation.1 | async-start | bytes 524288 | tf_op jit(solution)/shard_map/all_to_all | solution.py:28
  35.2 7.4 %all-to-all-start.2 = ((bf16[4,64,128]{2,1,0:T(8,128)(2,1)}), bf16[4,64,128]{2,1,0:T(8,128)(2,1)S(1)}, u32[]{:S(2)}, u32[]{:S(2)}) async-start(bf16[4,64,128]{2,1,0:T(8,128)(2,1)} %gather_fusion.6), calls=%async_computation.2 | async-start | bytes 131072 | tf_op jit(solution)/shard_map/all_to_all | solution.py:19
  42.6 13.5 %all-to-all-start.3 = ((bf16[16,64,128]{2,1,0:T(8,128)(2,1)}), bf16[16,64,128]{2,1,0:T(8,128)(2,1)S(1)}, u32[]{:S(2)}, u32[]{:S(2)}) async-start(bf16[16,64,128]{2,1,0:T(8,128)(2,1)} %gather_fusion.8), calls=%async_computation.3 | async-start | bytes 524288 | tf_op jit(solution)/shard_map/all_to_all | solution.py:28
  62.0 7.4 %all-to-all-start.4 = ((bf16[4,64,128]{2,1,0:T(8,128)(2,1)}), bf16[4,64,128]{2,1,0:T(8,128)(2,1)S(1)}, u32[]{:S(2)}, u32[]{:S(2)}) async-start(bf16[4,64,128]{2,1,0:T(8,128)(2,1)} %gather_fusion.11), calls=%async_computation.4 | async-start | bytes 131072 | tf_op jit(solution)/shard_map/all_to_all | solution.py:19
  69.4 13.5 %all-to-all-start.5 = ((bf16[16,64,128]{2,1,0:T(8,128)(2,1)}), bf16[16,64,128]{2,1,0:T(8,128)(2,1)S(1)}, u32[]{:S(2)}, u32[]{:S(2)}) async-start(bf16[16,64,128]{2,1,0:T(8,128)(2,1)} %gather_fusion.13), calls=%async_computation.5 | async-start | bytes 524288 | tf_op jit(solution)/shard_map/all_to_all | solution.py:28
  88.8 7.4 %all-to-all-start.6 = ((bf16[4,64,128]{2,1,0:T(8,128)(2,1)}), bf16[4,64,128]{2,1,0:T(8,128)(2,1)S(1)}, u32[]{:S(2)}, u32[]{:S(2)}) async-start(bf16[4,64,128]{2,1,0:T(8,128)(2,1)} %gather_fusion.16), calls=%async_computation.6 | async-start | bytes 131072 | tf_op jit(solution)/shard_map/all_to_all | solution.py:19
  96.2 13.5 %all-to-all-start.7 = ((bf16[16,64,128]{2,1,0:T(8,128)(2,1)}), bf16[16,64,128]{2,1,0:T(8,128)(2,1)S(1)}, u32[]{:S(2)}, u32[]{:S(2)}) async-start(bf16[16,64,128]{2,1,0:T(8,128)(2,1)} %gather_fusion.18), calls=%async_computation.7 | async-start | bytes 524288 | tf_op jit(solution)/shard_map/all_to_all | solution.py:28
  115.9 7.4 %all-to-all-start.8 = ((bf16[4,64,128]{2,1,0:T(8,128)(2,1)}), bf16[4,64,128]{2,1,0:T(8,128)(2,1)S(1)}, u32[]{:S(2)}, u32[]{:S(2)}) async-start(bf16[4,64,128]{2,1,0:T(8,128)(2,1)} %gather_fusion.21), calls=%async_computation.8 | async-start | bytes 131072 | tf_op jit(solution)/shard_map/all_to_all | solution.py:19
  123.3 13.5 %all-to-all-start.9 = ((bf16[16,64,128]{2,1,0:T(8,128)(2,1)}), bf16[16,64,128]{2,1,0:T(8,128)(2,1)S(1)}, u32[]{:S(2)}, u32[]{:S(2)}) async-start(bf16[16,64,128]{2,1,0:T(8,128)(2,1)} %gather_fusion.23), calls=%async_computation.9 | async-start | bytes 524288 | tf_op jit(solution)/shard_map/all_to_all | solution.py:28
  142.5 7.4 %all-to-all-start.10 = ((bf16[4,64,128]{2,1,0:T(8,128)(2,1)}), bf16[4,64,128]{2,1,0:T(8,128)(2,1)S(1)}, u32[]{:S(2)}, u32[]{:S(2)}) async-start(bf16[4,64,128]{2,1,0:T(8,128)(2,1)} %gather_fusion.26), calls=%async_computation.10 | async-start | bytes 131072 | tf_op jit(solution)/shard_map/all_to_all | solution.py:19
  150.0 13.5 %all-to-all-start.11 = ((bf16[16,64,128]{2,1,0:T(8,128)(2,1)}), bf16[16,64,128]{2,1,0:T(8,128)(2,1)S(1)}, u32[]{:S(2)}, u32[]{:S(2)}) async-start(bf16[16,64,128]{2,1,0:T(8,128)(2,1)} %gather_fusion.28), calls=%async_computation.11 | async-start | bytes 524288 | tf_op jit(solution)/shard_map/all_to_all | solution.py:28
  169.3 7.4 %all-to-all-start.12 = ((bf16[4,64,128]{2,1,0:T(8,128)(2,1)}), bf16[4,64,128]{2,1,0:T(8,128)(2,1)S(1)}, u32[]{:S(2)}, u32[]{:S(2)}) async-start(bf16[4,64,128]{2,1,0:T(8,128)(2,1)} %gather_fusion.31), calls=%async_computation.12 | async-start | bytes 131072 | tf_op jit(solution)/shard_map/all_to_all | solution.py:19
  176.7 13.5 %all-to-all-start.13 = ((bf16[16,64,128]{2,1,0:T(8,128)(2,1)}), bf16[16,64,128]{2,1,0:T(8,128)(2,1)S(1)}, u32[]{:S(2)}, u32[]{:S(2)}) async-start(bf16[16,64,128]{2,1,0:T(8,128)(2,1)} %gather_fusion.33), calls=%async_computation.13 | async-start | bytes 524288 | tf_op jit(solution)/shard_map/all_to_all | solution.py:28
  196.1 7.4 %all-to-all-start.14 = ((bf16[4,64,128]{2,1,0:T(8,128)(2,1)}), bf16[4,64,128]{2,1,0:T(8,128)(2,1)S(1)}, u32[]{:S(2)}, u32[]{:S(2)}) async-start(bf16[4,64,128]{2,1,0:T(8,128)(2,1)} %gather_fusion.36), calls=%async_computation.14 | async-start | bytes 131072 | tf_op jit(solution)/shard_map/all_to_all | solution.py:19
  203.5 13.5 %all-to-all-start.15 = ((bf16[16,64,128]{2,1,0:T(8,128)(2,1)}), bf16[16,64,128]{2,1,0:T(8,128)(2,1)S(1)}, u32[]{:S(2)}, u32[]{:S(2)}) async-start(bf16[16,64,128]{2,1,0:T(8,128)(2,1)} %gather_fusion.38), calls=%async_computation.15 | async-start | bytes 524288 | tf_op jit(solution)/shard_map/all_to_all | solution.py:28
where the time goes:
time: 224 us; the launch traced here: 222 us
  starting transfers between devices  58.6 us (26%)
  matrix products  58.5 us (26%)
  local copies, waits for them, and re-layouts  53.6 us (24%)
  waiting for transfers between devices  46.4 us (21%)
  other arithmetic  4.71 us (2%)
    all_to_all x8, waiting for transfers between devices, derivative(): lax.all_to_all(member_out, 'member', split_axis=0, concat_axis=0, tiled=T...  35.7 us
    all_to_all x8, starting transfers between devices, derivative(): lax.all_to_all(member_out, 'member', split_axis=0, concat_axis=0, tiled=T...  31.3 us
    all_to_all x8, starting transfers between devices, derivative(): lax.all_to_all(group_out, 'group', split_axis=0, concat_axis=0, tiled=True)  27.3 us
    dot_general x8, matrix products, derivative(): jnp.einsum('iktc,ikcd->itd', taken, blocks[:, 1:1 + members], preferred_e...  24.5 us
    dot_general x8, matrix products, derivative(): jnp.einsum('iktc,ikcd->itd', far_rows, blocks[:, 1 + members:], preferred...  17.6 us
    dot_general x8, matrix products, derivative(): jnp.einsum('itc,icd->itd', own_rows, blocks[:, 0], preferred_element_type...  16.4 us
    gather x8, local copies, waits for them, and re-layouts, derivative(): lax.all_to_all(member_out, 'member', split_axis=0, concat_axis=0, tiled=T...  13.2 us
    all_to_all x8, waiting for transfers between devices, derivative(): lax.all_to_all(group_out, 'group', split_axis=0, concat_axis=0, tiled=True)  10.8 us
  transfers between devices with their start and end apart: 16, of which 15 were waited for; matrix products, arithmetic and copies ran while one was open for 30% of the time, Pallas kernels for 0%

commit v1 on v0

v1 whole, which is shorter than its diff:
```python
import functools

import jax
import jax.numpy as jnp
from jax import lax
from jax.experimental import pallas as pl
from jax.experimental.pallas import tpu as pltpu
from jax.sharding import PartitionSpec as P

STEPS = 2
PIECES = 1
VMEM_LIMIT = 16 * 2**20


step_size = 0.1

VMEM = pl.BlockSpec(memory_space=pltpu.VMEM)
SMEM = pl.BlockSpec(memory_space=pltpu.SMEM)


class Sizes:
    def __init__(self, mesh, state, member_col, group_col, member_send, group_send):
        self.groups = mesh.shape["group"]
        self.members = mesh.shape["member"]
        self.rows, self.traj, self.cells = state.shape
        self.near = member_col.shape[1]
        self.far = group_col.shape[1]
        self.sent = group_send.shape[1] // self.groups
        self.piece = self.traj // PIECES
        self.at_own = 0
        self.at_near = self.at_own + self.rows
        self.at_far = self.at_near + self.rows * self.near
        self.at_msend = self.at_far + self.rows * self.far
        self.at_gsend = self.at_msend + self.members
        self.at_group = self.at_gsend + self.groups * self.sent


def group_row(sz, table, shift, slot):
    target = lax.rem(table[sz.at_group] + shift, sz.groups)
    return table[sz.at_gsend + target * sz.sent + slot]


def fill_sends(sz, table, rounded, member_out, group_out):
    for p in range(sz.members):
        member_out[p] = rounded[table[sz.at_msend + p]]
    for shift in range(1, sz.groups):
        for slot in range(sz.sent):
            group_out[(shift - 1) * sz.sent + slot] = rounded[group_row(sz, table, shift, slot)]


def first_kernel(sz, piece, table, state, rounded, member_out, group_out):
    span = pl.ds(piece * sz.piece, sz.piece)
    for i in range(sz.rows):
        rounded[i] = state[i, span].astype(jnp.bfloat16)
    fill_sends(sz, table, rounded, member_out, group_out)


def stage_kernel(sz, stage, last, base_span, *refs):
    it = iter(refs)
    table, blocks, rate, rounded, near, far = (next(it) for _ in range(6))
    base = next(it) if stage < 3 else None
    value = next(it) if stage > 0 else None
    total = next(it) if stage > 0 else None
    if not last:
        rounded_out, member_out, group_out = (next(it) for _ in range(3))
    out = next(it)
    total_out = next(it) if stage < 3 else None
    far_all = next(it)

    for slot in range(sz.sent):
        far_all[slot] = rounded[group_row(sz, table, 0, slot)]
    for j in range((sz.groups - 1) * sz.sent):
        far_all[sz.sent + j] = far[j]

    group = table[sz.at_group]
    for i in range(sz.rows):
        parts = [rounded[table[sz.at_own + i]]]
        for k in range(sz.near):
            parts.append(near[table[sz.at_near + i * sz.near + k]])
        for k in range(sz.far):
            col = table[sz.at_far + i * sz.far + k]
            place = lax.rem(group + sz.groups - lax.div(col, sz.sent), sz.groups)
            parts.append(far_all[place * sz.sent + lax.rem(col, sz.sent)])
        left = jnp.concatenate(parts, axis=1)
        product = jnp.dot(left, blocks[i], preferred_element_type=jnp.float32)
        start = base[i, base_span] if stage < 3 else None
        v = start if stage == 0 else value[i]
        slope = rate[i : i + 1] * (v - v * v * v) - product
        if stage < 3:
            ahead = 0.5 * step_size if stage < 2 else step_size
            weight = step_size / 6.0 if stage == 0 else step_size / 3.0
            fresh = start + ahead * slope
            total_out[i] = (start if stage == 0 else total[i]) + weight * slope
        else:
            fresh = total[i] + (step_size / 6.0) * slope
        out[i] = fresh
        if not last:
            rounded_out[i] = fresh.astype(jnp.bfloat16)
    if not last:
        fill_sends(sz, table, rounded_out, member_out, group_out)


def solution(mesh):
    def per_device(state, blocks, rate, own_col, member_col, group_col, member_send, group_send):
        sz = Sizes(mesh, state, member_col, group_col, member_send, group_send)
        table = jnp.concatenate(
            [
                own_col.reshape(-1),
                member_col.reshape(-1),
                group_col.reshape(-1),
                member_send.reshape(-1),
                group_send.reshape(-1),
                lax.axis_index("group").astype(jnp.int32).reshape(1),
            ]
        )
        weights = blocks.reshape(sz.rows, -1, sz.cells)
        f32 = jax.ShapeDtypeStruct((sz.rows, sz.piece, sz.cells), jnp.float32)
        bf16 = lambda n: jax.ShapeDtypeStruct((n, sz.piece, sz.cells), jnp.bfloat16)
        sends = [bf16(sz.rows), bf16(sz.members), bf16((sz.groups - 1) * sz.sent)]
        flops = 2 * sz.rows * weights.shape[1] * sz.cells * sz.piece

        def exchange(member_out, group_out):
            far = []
            for shift in range(1, sz.groups):
                pairs = [(g, (g + shift) % sz.groups) for g in range(sz.groups)]
                sent = group_out[(shift - 1) * sz.sent : shift * sz.sent]
                far.append(lax.ppermute(sent, "group", pairs))
            far = far[0] if len(far) == 1 else jnp.concatenate(far, axis=0)
            member_out, far = lax.optimization_barrier((member_out, far))
            near = lax.all_to_all(member_out, "member", split_axis=0, concat_axis=0, tiled=True)
            return near, far

        def begin(piece):
            return pl.pallas_call(
                functools.partial(first_kernel, sz, piece),
                out_shape=sends,
                in_specs=[SMEM, VMEM],
                out_specs=[VMEM] * 3,
                compiler_params=pltpu.CompilerParams(vmem_limit_bytes=VMEM_LIMIT),
                name="begin",
            )(table, state)

        def advance(stage, last, piece, carry, near, far):
            rounded, base, value, total = carry
            whole = base.shape[1] == sz.traj
            span = pl.ds(piece * sz.piece if whole else 0, sz.piece)
            ops = [table, weights, rate, rounded, near, far]
            if stage < 3:
                ops.append(base)
            if stage > 0:
                ops += [value, total]
            outs = ([] if last else list(sends)) + [f32] + ([f32] if stage < 3 else [])
            got = pl.pallas_call(
                functools.partial(stage_kernel, sz, stage, last, span),
                out_shape=outs,
                in_specs=[SMEM] + [VMEM] * (len(ops) - 1),
                out_specs=[VMEM] * len(outs),
                scratch_shapes=[pltpu.VMEM((sz.groups * sz.sent, sz.piece, sz.cells), jnp.bfloat16)],
                compiler_params=pltpu.CompilerParams(vmem_limit_bytes=VMEM_LIMIT),
                cost_estimate=pl.CostEstimate(flops=flops, bytes_accessed=weights.size * 2, transcendentals=0),
                name="stage",
            )(*ops)
            if last:
                return got[0], None, None
            if stage < 3:
                return (got[0], base, got[3], got[4]), got[1], got[2]
            return (got[0], got[3], None, None), got[1], got[2]

        carries, outgoing = [], []
        for piece in range(PIECES):
            rounded, member_out, group_out = begin(piece)
            carries.append((rounded, state, None, None))
            outgoing.append((member_out, group_out))
        for step in range(STEPS):
            for stage in range(4):
                last = step == STEPS - 1 and stage == 3
                for piece in range(PIECES):
                    near, far = exchange(*outgoing[piece])
                    carry, member_out, group_out = advance(stage, last, piece, carries[piece], near, far)
                    carries[piece] = carry
                    outgoing[piece] = (member_out, group_out)
        return carries[0] if PIECES == 1 else jnp.concatenate(carries, axis=1)

    return jax.shard_map(
        per_device,
        mesh=mesh,
        in_specs=(
            P(("group", "member"), None, None),
            P(("group", "member"), None, None, None),
            P(("group", "member"), None),
            P(("group", "member")),
            P(("group", "member"), None),
            P(("group", "member"), None),
            P(("group", "member"), None),
            P(("group", "member"), None),
        ),
        out_specs=P(("group", "member"), None, None),
        check_vma=False,
    )
```

time: 224 us -> 156 us (0.70)
  blocking collectives: 0 us -> 105 us
  matrix products: 58.5 us -> 0 us
  local copies, waits for them, and re-layouts: 53.6 us -> 5.28 us
  starting transfers between devices: 58.6 us -> 14.1 us
  waiting for transfers between devices: 46.4 us -> 18.7 us
  Pallas kernels: 0 us -> 12 us
  other arithmetic: 4.71 us -> 0 us
    all_to_all x0 -> x8, blocking collectives: none -> 105 us  [exchange(): lax.all_to_all(member_out, 'member', split_axis=0, concat_axis=0, tiled=T...]
    all_to_all x16 -> x0, starting transfers between devices: 58.6 us -> none  [the longest x8 31.3 us: derivative(): lax.all_to_all(member_out, 'member', split_axis=0, concat_axis=0, tiled=T...]
    dot_general x24 -> x0, matrix products: 58.5 us -> none  [the longest x8 24.5 us: derivative(): jnp.einsum('iktc,ikcd->itd', taken, blocks[:, 1:1 + members], preferred_e...]
    gather x40 -> x0, local copies, waits for them, and re-layouts: 53.4 us -> none  [the longest x8 13.2 us: derivative(): lax.all_to_all(member_out, 'member', split_axis=0, concat_axis=0, tiled=T...]
    all_to_all x16 -> x0, waiting for transfers between devices: 46.4 us -> none  [the longest x8 35.7 us: derivative(): lax.all_to_all(member_out, 'member', split_axis=0, concat_axis=0, tiled=T...]
    ppermute x0 -> x8, waiting for transfers between devices: none -> 18.7 us  [exchange(): far.append(lax.ppermute(sent, 'group', pairs))]
    ppermute x0 -> x8, starting transfers between devices: none -> 14.1 us  [exchange(): far.append(lax.ppermute(sent, 'group', pairs))]
    pallas_call x0 -> x9, Pallas kernels: none -> 12 us  [the longest x8 11.4 us: advance(): pl.pallas_call(functools.partial(stage_kernel, sz, stage, last, span), ou...]
  transfers between devices with their start and end apart: 16 -> 8, of which waited for: 15 -> 8; matrix products, arithmetic and copies ran while one was open for 30% -> 0% of each run, Pallas kernels for 0% -> 0%
where the time goes in v1:
time: 156 us; the launch traced here: 155 us
  blocking collectives  105 us (67%)
  waiting for transfers between devices  18.7 us (12%)
  starting transfers between devices  14.1 us (9%)
  Pallas kernels  12 us (8%)
  local copies, waits for them, and re-layouts  5.28 us (3%)
    all_to_all x8, blocking collectives, exchange(): lax.all_to_all(member_out, 'member', split_axis=0, concat_axis=0, tiled=T...  105 us
    ppermute x8, waiting for transfers between devices, exchange(): far.append(lax.ppermute(sent, 'group', pairs))  18.7 us
    ppermute x8, starting transfers between devices, exchange(): far.append(lax.ppermute(sent, 'group', pairs))  14.1 us
    pallas_call x8, Pallas kernels, advance(): pl.pallas_call(functools.partial(stage_kernel, sz, stage, last, span), ou...  11.4 us
    unnamed x11, local copies, waits for them, and re-layouts  4.41 us
  transfers between devices with their start and end apart: 8, of which 8 were waited for; matrix products, arithmetic and copies ran while one was open for 0% of the time, Pallas kernels for 0%

profile of v1, /device:TPU:0, one launch (start us, length us, event | category | flops | bytes accessed | tf_op | source)
XLA Modules:
  0.0 155.1 jit_solution(15463891658741529350)
XLA Ops:
  0.0 0.0 copy-start.4
  0.0 0.8 copy.10
  0.8 0.1 reshape.18
  0.9 0.8 concatenate.3.table.refs_0_
  1.6 0.0 copy-start.2
  1.6 1.0 copy-done.2
  2.7 0.6 begin.1
  3.3 3.1 %collective-permute-start = (bf16[2,64,128]{2,1,0:T(8,128)(2,1)S(1)}, bf16[2,64,128]{2,1,0:T(8,128)(2,1)S(1)}, u32[]{:S(2)}, u32[]{:S(2)}) collective-permute-start(bf16[2,64,128]{2,1,0:T(8,128)(2,1)S(1)} %get-tuple-element.60), channel_id=1, source_target_pairs={{0,16},{16,0},{1,17},{17,1},{2,18},{18,2},{3,19},{19,3},{4,20},{20... | collective-permute-start | bytes 98312 | tf_op jit(solution)/shard_map/ppermute | solution.py:127
  6.3 1.9 %collective-permute-done.refs_5_ = bf16[2,64,128]{2,1,0:T(8,128)(2,1)S(1)} collective-permute-done((bf16[2,64,128]{2,1,0:T(8,128)(2,1)S(1)}, bf16[2,64,128]{2,1,0:T(8,128)(2,1)S(1)}, u32[]{:S(2)}, u32[]{:S(2)}) %collective-permute-start) | collective-permute-done | bytes 32800 | tf_op jit(solution)/shard_map/ppermute | solution.py:127
  8.2 16.2 %all_to_all.40.refs_4_ = bf16[16,64,128]{2,1,0:T(8,128)(2,1)S(1)} all-to-all(bf16[16,64,128]{2,1,0:T(8,128)(2,1)S(1)} %get-tuple-element.61), channel_id=1, replica_groups=mesh['group'=2,'member'=16] {'member'}, dimensions={0} | all-to-all | bytes 524288 | tf_op jit(solution)/shard_map/all_to_all | solution.py:130
  24.5 0.0 copy-start
  24.5 1.9 %copy-done = bf16[16,6,128,128]{3,2,1,0:T(8,128)(2,1)S(1)} copy-done((bf16[16,6,128,128]{3,2,1,0:T(8,128)(2,1)S(1)}, bf16[16,6,128,128]{3,2,1,0:T(8,128)(2,1)}, u32[]{:S(2)}) %copy-start) | copy-done | bytes 3145752
  26.3 0.0 copy-start.3
  26.3 0.7 copy-done.3
  27.0 0.0 copy-start.1
  27.0 1.3 stage.8
  28.4 1.6 %collective-permute-start.1 = (bf16[2,64,128]{2,1,0:T(8,128)(2,1)S(1)}, bf16[2,64,128]{2,1,0:T(8,128)(2,1)S(1)}, u32[]{:S(2)}, u32[]{:S(2)}) collective-permute-start(bf16[2,64,128]{2,1,0:T(8,128)(2,1)S(1)} %get-tuple-element.65), channel_id=1, source_target_pairs={{0,16},{16,0},{1,17},{17,1},{2,18},{18,2},{3,19},{19,3},{4,20},{20... | collective-permute-start | bytes 98312 | tf_op jit(solution)/shard_map/ppermute | solution.py:127
  30.0 2.4 %collective-permute-done.1.refs_5_ = bf16[2,64,128]{2,1,0:T(8,128)(2,1)S(1)} collective-permute-done((bf16[2,64,128]{2,1,0:T(8,128)(2,1)S(1)}, bf16[2,64,128]{2,1,0:T(8,128)(2,1)S(1)}, u32[]{:S(2)}, u32[]{:S(2)}) %collective-permute-start.1) | collective-permute-done | bytes 32800 | tf_op jit(solution)/shard_map/ppermute | solution.py:127
  32.4 12.7 %all_to_all.41.refs_4_ = bf16[16,64,128]{2,1,0:T(8,128)(2,1)S(1)} all-to-all(bf16[16,64,128]{2,1,0:T(8,128)(2,1)S(1)} %get-tuple-element.66), channel_id=1, replica_groups=mesh['group'=2,'member'=16] {'member'}, dimensions={0} | all-to-all | bytes 524288 | tf_op jit(solution)/shard_map/all_to_all | solution.py:130
  45.0 0.0 copy-done.4
  45.1 0.0 copy-done.1
  45.1 1.3 stage.9
  46.4 1.6 %collective-permute-start.2 = (bf16[2,64,128]{2,1,0:T(8,128)(2,1)S(1)}, bf16[2,64,128]{2,1,0:T(8,128)(2,1)S(1)}, u32[]{:S(2)}, u32[]{:S(2)}) collective-permute-start(bf16[2,64,128]{2,1,0:T(8,128)(2,1)S(1)} %get-tuple-element.72), channel_id=1, source_target_pairs={{0,16},{16,0},{1,17},{17,1},{2,18},{18,2},{3,19},{19,3},{4,20},{20... | collective-permute-start | bytes 98312 | tf_op jit(solution)/shard_map/ppermute | solution.py:127
  48.0 2.4 %collective-permute-done.2.refs_5_ = bf16[2,64,128]{2,1,0:T(8,128)(2,1)S(1)} collective-permute-done((bf16[2,64,128]{2,1,0:T(8,128)(2,1)S(1)}, bf16[2,64,128]{2,1,0:T(8,128)(2,1)S(1)}, u32[]{:S(2)}, u32[]{:S(2)}) %collective-permute-start.2) | collective-permute-done | bytes 32800 | tf_op jit(solution)/shard_map/ppermute | solution.py:127
  50.4 12.7 %all_to_all.42.refs_4_ = bf16[16,64,128]{2,1,0:T(8,128)(2,1)S(1)} all-to-all(bf16[16,64,128]{2,1,0:T(8,128)(2,1)S(1)} %get-tuple-element.73), channel_id=1, replica_groups=mesh['group'=2,'member'=16] {'member'}, dimensions={0} | all-to-all | bytes 524288 | tf_op jit(solution)/shard_map/all_to_all | solution.py:130
  63.1 1.3 stage.10
  64.4 1.6 %collective-permute-start.3 = (bf16[2,64,128]{2,1,0:T(8,128)(2,1)S(1)}, bf16[2,64,128]{2,1,0:T(8,128)(2,1)S(1)}, u32[]{:S(2)}, u32[]{:S(2)}) collective-permute-start(bf16[2,64,128]{2,1,0:T(8,128)(2,1)S(1)} %get-tuple-element.79), channel_id=1, source_target_pairs={{0,16},{16,0},{1,17},{17,1},{2,18},{18,2},{3,19},{19,3},{4,20},{20... | collective-permute-start | bytes 98312 | tf_op jit(solution)/shard_map/ppermute | solution.py:127
  66.0 2.4 %collective-permute-done.3.refs_5_ = bf16[2,64,128]{2,1,0:T(8,128)(2,1)S(1)} collective-permute-done((bf16[2,64,128]{2,1,0:T(8,128)(2,1)S(1)}, bf16[2,64,128]{2,1,0:T(8,128)(2,1)S(1)}, u32[]{:S(2)}, u32[]{:S(2)}) %collective-permute-start.3) | collective-permute-done | bytes 32800 | tf_op jit(solution)/shard_map/ppermute | solution.py:127
  68.4 12.7 %all_to_all.43.refs_4_ = bf16[16,64,128]{2,1,0:T(8,128)(2,1)S(1)} all-to-all(bf16[16,64,128]{2,1,0:T(8,128)(2,1)S(1)} %get-tuple-element.80), channel_id=1, replica_groups=mesh['group'=2,'member'=16] {'member'}, dimensions={0} | all-to-all | bytes 524288 | tf_op jit(solution)/shard_map/all_to_all | solution.py:130
  81.0 1.3 stage.11
  82.4 1.6 %collective-permute-start.4 = (bf16[2,64,128]{2,1,0:T(8,128)(2,1)S(1)}, bf16[2,64,128]{2,1,0:T(8,128)(2,1)S(1)}, u32[]{:S(2)}, u32[]{:S(2)}) collective-permute-start(bf16[2,64,128]{2,1,0:T(8,128)(2,1)S(1)} %get-tuple-element.86), channel_id=1, source_target_pairs={{0,16},{16,0},{1,17},{17,1},{2,18},{18,2},{3,19},{19,3},{4,20},{20... | collective-permute-start | bytes 98312 | tf_op jit(solution)/shard_map/ppermute | solution.py:127
  84.0 2.4 %collective-permute-done.4.refs_5_ = bf16[2,64,128]{2,1,0:T(8,128)(2,1)S(1)} collective-permute-done((bf16[2,64,128]{2,1,0:T(8,128)(2,1)S(1)}, bf16[2,64,128]{2,1,0:T(8,128)(2,1)S(1)}, u32[]{:S(2)}, u32[]{:S(2)}) %collective-permute-start.4) | collective-permute-done | bytes 32800 | tf_op jit(solution)/shard_map/ppermute | solution.py:127
  86.4 12.7 %all_to_all.44.refs_4_ = bf16[16,64,128]{2,1,0:T(8,128)(2,1)S(1)} all-to-all(bf16[16,64,128]{2,1,0:T(8,128)(2,1)S(1)} %get-tuple-element.87), channel_id=1, replica_groups=mesh['group'=2,'member'=16] {'member'}, dimensions={0} | all-to-all | bytes 524288 | tf_op jit(solution)/shard_map/all_to_all | solution.py:130
  99.0 1.3 stage.12
  100.4 1.6 %collective-permute-start.5 = (bf16[2,64,128]{2,1,0:T(8,128)(2,1)S(1)}, bf16[2,64,128]{2,1,0:T(8,128)(2,1)S(1)}, u32[]{:S(2)}, u32[]{:S(2)}) collective-permute-start(bf16[2,64,128]{2,1,0:T(8,128)(2,1)S(1)} %get-tuple-element.92), channel_id=1, source_target_pairs={{0,16},{16,0},{1,17},{17,1},{2,18},{18,2},{3,19},{19,3},{4,20},{20... | collective-permute-start | bytes 98312 | tf_op jit(solution)/shard_map/ppermute | solution.py:127
  102.0 2.4 %collective-permute-done.5.refs_5_ = bf16[2,64,128]{2,1,0:T(8,128)(2,1)S(1)} collective-permute-done((bf16[2,64,128]{2,1,0:T(8,128)(2,1)S(1)}, bf16[2,64,128]{2,1,0:T(8,128)(2,1)S(1)}, u32[]{:S(2)}, u32[]{:S(2)}) %collective-permute-start.5) | collective-permute-done | bytes 32800 | tf_op jit(solution)/shard_map/ppermute | solution.py:127
  104.4 12.7 %all_to_all.45.refs_4_ = bf16[16,64,128]{2,1,0:T(8,128)(2,1)S(1)} all-to-all(bf16[16,64,128]{2,1,0:T(8,128)(2,1)S(1)} %get-tuple-element.93), channel_id=1, replica_groups=mesh['group'=2,'member'=16] {'member'}, dimensions={0} | all-to-all | bytes 524288 | tf_op jit(solution)/shard_map/all_to_all | solution.py:130
  117.0 1.3 stage.13
  118.4 1.6 %collective-permute-start.6 = (bf16[2,64,128]{2,1,0:T(8,128)(2,1)S(1)}, bf16[2,64,128]{2,1,0:T(8,128)(2,1)S(1)}, u32[]{:S(2)}, u32[]{:S(2)}) collective-permute-start(bf16[2,64,128]{2,1,0:T(8,128)(2,1)S(1)} %get-tuple-element.99), channel_id=1, source_target_pairs={{0,16},{16,0},{1,17},{17,1},{2,18},{18,2},{3,19},{19,3},{4,20},{20... | collective-permute-start | bytes 98312 | tf_op jit(solution)/shard_map/ppermute | solution.py:127
  119.9 2.4 %collective-permute-done.6.refs_5_ = bf16[2,64,128]{2,1,0:T(8,128)(2,1)S(1)} collective-permute-done((bf16[2,64,128]{2,1,0:T(8,128)(2,1)S(1)}, bf16[2,64,128]{2,1,0:T(8,128)(2,1)S(1)}, u32[]{:S(2)}, u32[]{:S(2)}) %collective-permute-start.6) | collective-permute-done | bytes 32800 | tf_op jit(solution)/shard_map/ppermute | solution.py:127
  122.4 12.7 %all_to_all.46.refs_4_ = bf16[16,64,128]{2,1,0:T(8,128)(2,1)S(1)} all-to-all(bf16[16,64,128]{2,1,0:T(8,128)(2,1)S(1)} %get-tuple-element.100), channel_id=1, replica_groups=mesh['group'=2,'member'=16] {'member'}, dimensions={0} | all-to-all | bytes 524288 | tf_op jit(solution)/shard_map/all_to_all | solution.py:130
  135.0 1.3 stage.14
  136.4 1.6 %collective-permute-start.7 = (bf16[2,64,128]{2,1,0:T(8,128)(2,1)S(1)}, bf16[2,64,128]{2,1,0:T(8,128)(2,1)S(1)}, u32[]{:S(2)}, u32[]{:S(2)}) collective-permute-start(bf16[2,64,128]{2,1,0:T(8,128)(2,1)S(1)} %get-tuple-element.106), channel_id=1, source_target_pairs={{0,16},{16,0},{1,17},{17,1},{2,18},{18,2},{3,19},{19,3},{4,20},{20... | collective-permute-start | bytes 98312 | tf_op jit(solution)/shard_map/ppermute | solution.py:127
  137.9 2.4 %collective-permute-done.7.refs_5_ = bf16[2,64,128]{2,1,0:T(8,128)(2,1)S(1)} collective-permute-done((bf16[2,64,128]{2,1,0:T(8,128)(2,1)S(1)}, bf16[2,64,128]{2,1,0:T(8,128)(2,1)S(1)}, u32[]{:S(2)}, u32[]{:S(2)}) %collective-permute-start.7) | collective-permute-done | bytes 32800 | tf_op jit(solution)/shard_map/ppermute | solution.py:127
  140.3 12.7 %all_to_all.47.refs_4_ = bf16[16,64,128]{2,1,0:T(8,128)(2,1)S(1)} all-to-all(bf16[16,64,128]{2,1,0:T(8,128)(2,1)S(1)} %get-tuple-element.107), channel_id=1, replica_groups=mesh['group'=2,'member'=16] {'member'}, dimensions={0} | all-to-all | bytes 524288 | tf_op jit(solution)/shard_map/all_to_all | solution.py:130
  153.0 2.1 %stage.15 = f32[16,64,128]{2,1,0:T(8,128)} custom-call(s32[117]{0:T(128)S(1)} %concatenate.3.table.refs_0_, bf16[16,768,128]{2,1,0:T(8,128)(2,1)S(1)} %bitcast.12, f32[16,128]{1,0:T(8,128)S(1)} %copy-done.4, bf16[16,64,128]{2,1,0:T(8,128)(2,1)S(1)} %get-tuple-element.104.refs_3_, bf16[16,64,128]{2,1,0:T(8,128)(2,1)S(1)} %all_to_all.47.refs_4_, ...), custom_call_target="tpu_custom_call" | custom-call | flops 201326592 | bytes 3145728 | tf_op jit(solution)/shard_map/stage/pallas_call | solution.py:153
Async XLA Ops:
  0.0 45.0 %copy-start.4 = (f32[16,128]{1,0:T(8,128)S(1)}, f32[16,128]{1,0:T(8,128)}, u32[]{:S(2)}) copy-start(f32[16,128]{1,0:T(8,128)} %refs_2_.15) | copy-start | bytes 24580
  1.6 1.0 copy-start.2
  3.3 5.0 %collective-permute-start = (bf16[2,64,128]{2,1,0:T(8,128)(2,1)S(1)}, bf16[2,64,128]{2,1,0:T(8,128)(2,1)S(1)}, u32[]{:S(2)}, u32[]{:S(2)}) collective-permute-start(bf16[2,64,128]{2,1,0:T(8,128)(2,1)S(1)} %get-tuple-element.60), channel_id=1, source_target_pairs={{0,16},{16,0},{1,17},{17,1},{2,18},{18,2},{3,19},{19,3},{4,20},{20... | collective-permute-start | bytes 98312 | tf_op jit(solution)/shard_map/ppermute | solution.py:127
  24.5 1.9 %copy-start = (bf16[16,6,128,128]{3,2,1,0:T(8,128)(2,1)S(1)}, bf16[16,6,128,128]{3,2,1,0:T(8,128)(2,1)}, u32[]{:S(2)}) copy-start(bf16[16,6,128,128]{3,2,1,0:T(8,128)(2,1)} %param.9) | copy-start | bytes 9437188
  26.3 0.7 copy-start.3
  27.0 18.0 %copy-start.1 = (bf16[16,6,128,128]{3,2,1,0:T(8,128)(2,1)S(1)}, bf16[16,6,128,128]{3,2,1,0:T(8,128)(2,1)}, u32[]{:S(2)}) copy-start(bf16[16,6,128,128]{3,2,1,0:T(8,128)(2,1)} %param.9) | copy-start | bytes 9437188
  28.4 4.0 %collective-permute-start.1 = (bf16[2,64,128]{2,1,0:T(8,128)(2,1)S(1)}, bf16[2,64,128]{2,1,0:T(8,128)(2,1)S(1)}, u32[]{:S(2)}, u32[]{:S(2)}) collective-permute-start(bf16[2,64,128]{2,1,0:T(8,128)(2,1)S(1)} %get-tuple-element.65), channel_id=1, source_target_pairs={{0,16},{16,0},{1,17},{17,1},{2,18},{18,2},{3,19},{19,3},{4,20},{20... | collective-permute-start | bytes 98312 | tf_op jit(solution)/shard_map/ppermute | solution.py:127
  46.4 4.0 %collective-permute-start.2 = (bf16[2,64,128]{2,1,0:T(8,128)(2,1)S(1)}, bf16[2,64,128]{2,1,0:T(8,128)(2,1)S(1)}, u32[]{:S(2)}, u32[]{:S(2)}) collective-permute-start(bf16[2,64,128]{2,1,0:T(8,128)(2,1)S(1)} %get-tuple-element.72), channel_id=1, source_target_pairs={{0,16},{16,0},{1,17},{17,1},{2,18},{18,2},{3,19},{19,3},{4,20},{20... | collective-permute-start | bytes 98312 | tf_op jit(solution)/shard_map/ppermute | solution.py:127
  64.4 4.0 %collective-permute-start.3 = (bf16[2,64,128]{2,1,0:T(8,128)(2,1)S(1)}, bf16[2,64,128]{2,1,0:T(8,128)(2,1)S(1)}, u32[]{:S(2)}, u32[]{:S(2)}) collective-permute-start(bf16[2,64,128]{2,1,0:T(8,128)(2,1)S(1)} %get-tuple-element.79), channel_id=1, source_target_pairs={{0,16},{16,0},{1,17},{17,1},{2,18},{18,2},{3,19},{19,3},{4,20},{20... | collective-permute-start | bytes 98312 | tf_op jit(solution)/shard_map/ppermute | solution.py:127
  82.4 4.0 %collective-permute-start.4 = (bf16[2,64,128]{2,1,0:T(8,128)(2,1)S(1)}, bf16[2,64,128]{2,1,0:T(8,128)(2,1)S(1)}, u32[]{:S(2)}, u32[]{:S(2)}) collective-permute-start(bf16[2,64,128]{2,1,0:T(8,128)(2,1)S(1)} %get-tuple-element.86), channel_id=1, source_target_pairs={{0,16},{16,0},{1,17},{17,1},{2,18},{18,2},{3,19},{19,3},{4,20},{20... | collective-permute-start | bytes 98312 | tf_op jit(solution)/shard_map/ppermute | solution.py:127
  100.4 4.0 %collective-permute-start.5 = (bf16[2,64,128]{2,1,0:T(8,128)(2,1)S(1)}, bf16[2,64,128]{2,1,0:T(8,128)(2,1)S(1)}, u32[]{:S(2)}, u32[]{:S(2)}) collective-permute-start(bf16[2,64,128]{2,1,0:T(8,128)(2,1)S(1)} %get-tuple-element.92), channel_id=1, source_target_pairs={{0,16},{16,0},{1,17},{17,1},{2,18},{18,2},{3,19},{19,3},{4,20},{20... | collective-permute-start | bytes 98312 | tf_op jit(solution)/shard_map/ppermute | solution.py:127
  118.4 4.0 %collective-permute-start.6 = (bf16[2,64,128]{2,1,0:T(8,128)(2,1)S(1)}, bf16[2,64,128]{2,1,0:T(8,128)(2,1)S(1)}, u32[]{:S(2)}, u32[]{:S(2)}) collective-permute-start(bf16[2,64,128]{2,1,0:T(8,128)(2,1)S(1)} %get-tuple-element.99), channel_id=1, source_target_pairs={{0,16},{16,0},{1,17},{17,1},{2,18},{18,2},{3,19},{19,3},{4,20},{20... | collective-permute-start | bytes 98312 | tf_op jit(solution)/shard_map/ppermute | solution.py:127
  136.4 4.0 %collective-permute-start.7 = (bf16[2,64,128]{2,1,0:T(8,128)(2,1)S(1)}, bf16[2,64,128]{2,1,0:T(8,128)(2,1)S(1)}, u32[]{:S(2)}, u32[]{:S(2)}) collective-permute-start(bf16[2,64,128]{2,1,0:T(8,128)(2,1)S(1)} %get-tuple-element.106), channel_id=1, source_target_pairs={{0,16},{16,0},{1,17},{17,1},{2,18},{18,2},{3,19},{19,3},{4,20},{20... | collective-permute-start | bytes 98312 | tf_op jit(solution)/shard_map/ppermute | solution.py:127

commit v2 on v1

--- a/solution.py
+++ b/solution.py
@@ -7,19 +7,21 @@
 from jax.experimental.pallas import tpu as pltpu
 from jax.sharding import PartitionSpec as P
 
+
 STEPS = 2
 PIECES = 1
-VMEM_LIMIT = 16 * 2**20
 
 
 step_size = 0.1
 
+
 VMEM = pl.BlockSpec(memory_space=pltpu.VMEM)
+ANY = pl.BlockSpec(memory_space=pl.ANY)
 SMEM = pl.BlockSpec(memory_space=pltpu.SMEM)
 
 
 class Sizes:
-    def __init__(self, mesh, state, member_col, group_col, member_send, group_send):
+    def __init__(self, mesh, state, member_col, group_col, group_send):
         self.groups = mesh.shape["group"]
         self.members = mesh.shape["member"]
         self.rows, self.traj, self.cells = state.shape
@@ -102,7 +104,7 @@
 
 def solution(mesh):
     def per_device(state, blocks, rate, own_col, member_col, group_col, member_send, group_send):
-        sz = Sizes(mesh, state, member_col, group_col, member_send, group_send)
+        sz = Sizes(mesh, state, member_col, group_col, group_send)
         table = jnp.concatenate(
             [
                 own_col.reshape(-1),
@@ -117,6 +119,7 @@
         f32 = jax.ShapeDtypeStruct((sz.rows, sz.piece, sz.cells), jnp.float32)
         bf16 = lambda n: jax.ShapeDtypeStruct((n, sz.piece, sz.cells), jnp.bfloat16)
         sends = [bf16(sz.rows), bf16(sz.members), bf16((sz.groups - 1) * sz.sent)]
+        limit = 16 * 2**20
         flops = 2 * sz.rows * weights.shape[1] * sz.cells * sz.piece
 
         def exchange(member_out, group_out):
@@ -125,10 +128,20 @@
                 pairs = [(g, (g + shift) % sz.groups) for g in range(sz.groups)]
                 sent = group_out[(shift - 1) * sz.sent : shift * sz.sent]
                 far.append(lax.ppermute(sent, "group", pairs))
-            far = far[0] if len(far) == 1 else jnp.concatenate(far, axis=0)
-            member_out, far = lax.optimization_barrier((member_out, far))
             near = lax.all_to_all(member_out, "member", split_axis=0, concat_axis=0, tiled=True)
-            return near, far
+            near = landed(near)
+            return near, far[0] if len(far) == 1 else jnp.concatenate(far, axis=0)
+
+        def landed(near):
+            return pl.pallas_call(
+                lambda near, same: None,
+                out_shape=near,
+                in_specs=[ANY],
+                out_specs=ANY,
+                input_output_aliases={0: 0},
+                compiler_params=pltpu.CompilerParams(vmem_limit_bytes=limit),
+                name="landed",
+            )(near)
 
         def begin(piece):
             return pl.pallas_call(
@@ -136,7 +149,7 @@
                 out_shape=sends,
                 in_specs=[SMEM, VMEM],
                 out_specs=[VMEM] * 3,
-                compiler_params=pltpu.CompilerParams(vmem_limit_bytes=VMEM_LIMIT),
+                compiler_params=pltpu.CompilerParams(vmem_limit_bytes=limit),
                 name="begin",
             )(table, state)
 
@@ -156,7 +169,7 @@
                 in_specs=[SMEM] + [VMEM] * (len(ops) - 1),
                 out_specs=[VMEM] * len(outs),
                 scratch_shapes=[pltpu.VMEM((sz.groups * sz.sent, sz.piece, sz.cells), jnp.bfloat16)],
-                compiler_params=pltpu.CompilerParams(vmem_limit_bytes=VMEM_LIMIT),
+                compiler_params=pltpu.CompilerParams(vmem_limit_bytes=limit),
                 cost_estimate=pl.CostEstimate(flops=flops, bytes_accessed=weights.size * 2, transcendentals=0),
                 name="stage",
             )(*ops)

time: 156 us -> 180 us (1.15)
  blocking collectives: 105 us -> 0 us
  waiting for transfers between devices: 18.7 us -> 67.2 us
  local copies, waits for them, and re-layouts: 5.28 us -> 52.6 us
  starting transfers between devices: 14.1 us -> 45 us
    all_to_all x8 -> x0, blocking collectives: 105 us -> none  [exchange(): lax.all_to_all(member_out, 'member', split_axis=0, concat_axis=0, tiled=T...]
    all_to_all x0 -> x8, waiting for transfers between devices: none -> 67.1 us  [exchange(): lax.all_to_all(member_out, 'member', split_axis=0, concat_axis=0, tiled=T...]
    unnamed x11 -> x119, local copies, waits for them, and re-layouts: 4.41 us -> 51.8 us
    all_to_all x0 -> x8, starting transfers between devices: none -> 32.2 us  [exchange(): lax.all_to_all(member_out, 'member', split_axis=0, concat_axis=0, tiled=T...]
    ppermute x8, waiting for transfers between devices: 18.7 us -> 0.02 us  [exchange(): far.append(lax.ppermute(sent, 'group', pairs))]
  transfers between devices with their start and end apart: 8 -> 16, of which waited for: 8 -> 8; matrix products, arithmetic and copies ran while one was open for 0% -> 0% of each run, Pallas kernels for 0% -> 0%
where the time goes in v2:
time: 180 us; the launch traced here: 178 us
  waiting for transfers between devices  67.2 us (37%)
  local copies, waits for them, and re-layouts  52.6 us (29%)
  starting transfers between devices  45 us (25%)
  Pallas kernels  12.7 us (7%)
    all_to_all x8, waiting for transfers between devices, exchange(): lax.all_to_all(member_out, 'member', split_axis=0, concat_axis=0, tiled=T...  67.1 us
    unnamed x119, local copies, waits for them, and re-layouts  51.8 us
    all_to_all x8, starting transfers between devices, exchange(): lax.all_to_all(member_out, 'member', split_axis=0, concat_axis=0, tiled=T...  32.2 us
    ppermute x8, starting transfers between devices, exchange(): far.append(lax.ppermute(sent, 'group', pairs))  12.7 us
    pallas_call x8, Pallas kernels, advance(): pl.pallas_call(functools.partial(stage_kernel, sz, stage, last, span), ou...  11.4 us
  transfers between devices with their start and end apart: 16, of which 8 were waited for; matrix products, arithmetic and copies ran while one was open for 0% of the time, Pallas kernels for 0%

profile of v2, /device:TPU:0, one launch (start us, length us, event | category | flops | bytes accessed | tf_op | source)
XLA Modules:
  0.0 177.7 jit_solution(6976074619680925401)
XLA Ops:
  1.6 1.0 copy-done.2
  2.7 1.3 begin.1
  4.7 7.5 %all-to-all-start = ((bf16[16,64,128]{2,1,0:T(8,128)(2,1)}), bf16[16,64,128]{2,1,0:T(8,128)(2,1)S(1)}, u32[]{:S(2)}, u32[]{:S(2)}) async-start(bf16[16,64,128]{2,1,0:T(8,128)(2,1)} %get-tuple-element.43), calls=%async_computation | async-start | bytes 524288 | tf_op jit(solution)/shard_map/all_to_all | solution.py:131
  12.2 1.6 collective-permute-start
  13.8 8.4 %all-to-all-done.near = bf16[16,64,128]{2,1,0:T(8,128)(2,1)S(1)} async-done(((bf16[16,64,128]{2,1,0:T(8,128)(2,1)}), bf16[16,64,128]{2,1,0:T(8,128)(2,1)S(1)}, u32[]{:S(2)}, u32[]{:S(2)}) %all-to-all-start) | async-done | bytes 262176 | tf_op jit(solution)/shard_map/all_to_all | solution.py:131
  22.2 1.9 %copy-done = bf16[16,6,128,128]{3,2,1,0:T(8,128)(2,1)S(1)} copy-done((bf16[16,6,128,128]{3,2,1,0:T(8,128)(2,1)S(1)}, bf16[16,6,128,128]{3,2,1,0:T(8,128)(2,1)}, u32[]{:S(2)}) %copy-start) | copy-done | bytes 3145752
  26.8 1.3 stage.8
  31.2 3.5 %all-to-all-start.1 = ((bf16[16,64,128]{2,1,0:T(8,128)(2,1)}), bf16[16,64,128]{2,1,0:T(8,128)(2,1)S(1)}, u32[]{:S(2)}, u32[]{:S(2)}) async-start(bf16[16,64,128]{2,1,0:T(8,128)(2,1)} %copy-done.57), calls=%async_computation.1 | async-start | bytes 524288 | tf_op jit(solution)/shard_map/all_to_all | solution.py:131
  34.7 1.6 collective-permute-start.1
  36.3 8.4 %all-to-all-done.1.near = bf16[16,64,128]{2,1,0:T(8,128)(2,1)S(1)} async-done(((bf16[16,64,128]{2,1,0:T(8,128)(2,1)}), bf16[16,64,128]{2,1,0:T(8,128)(2,1)S(1)}, u32[]{:S(2)}, u32[]{:S(2)}) %all-to-all-start.1) | async-done | bytes 262176 | tf_op jit(solution)/shard_map/all_to_all | solution.py:131
  45.8 1.0 copy-done.25
  46.8 1.0 copy-done.27
  48.8 1.3 stage.9
  53.1 3.5 %all-to-all-start.2 = ((bf16[16,64,128]{2,1,0:T(8,128)(2,1)}), bf16[16,64,128]{2,1,0:T(8,128)(2,1)S(1)}, u32[]{:S(2)}, u32[]{:S(2)}) async-start(bf16[16,64,128]{2,1,0:T(8,128)(2,1)} %copy-done.53), calls=%async_computation.2 | async-start | bytes 524288 | tf_op jit(solution)/shard_map/all_to_all | solution.py:131
  56.7 1.6 collective-permute-start.2
  58.3 8.4 %all-to-all-done.2.near = bf16[16,64,128]{2,1,0:T(8,128)(2,1)S(1)} async-done(((bf16[16,64,128]{2,1,0:T(8,128)(2,1)}), bf16[16,64,128]{2,1,0:T(8,128)(2,1)S(1)}, u32[]{:S(2)}, u32[]{:S(2)}) %all-to-all-start.2) | async-done | bytes 262176 | tf_op jit(solution)/shard_map/all_to_all | solution.py:131
  66.7 1.0 copy-done.5
  67.7 1.0 copy-done.21
  68.8 1.0 copy-done.23
  70.7 1.3 stage.10
  75.1 3.5 %all-to-all-start.3 = ((bf16[16,64,128]{2,1,0:T(8,128)(2,1)}), bf16[16,64,128]{2,1,0:T(8,128)(2,1)S(1)}, u32[]{:S(2)}, u32[]{:S(2)}) async-start(bf16[16,64,128]{2,1,0:T(8,128)(2,1)} %copy-done.54), calls=%async_computation.3 | async-start | bytes 524288 | tf_op jit(solution)/shard_map/all_to_all | solution.py:131
  78.6 1.6 collective-permute-start.3
  80.2 8.4 %all-to-all-done.3.near = bf16[16,64,128]{2,1,0:T(8,128)(2,1)S(1)} async-done(((bf16[16,64,128]{2,1,0:T(8,128)(2,1)}), bf16[16,64,128]{2,1,0:T(8,128)(2,1)S(1)}, u32[]{:S(2)}, u32[]{:S(2)}) %all-to-all-start.3) | async-done | bytes 262176 | tf_op jit(solution)/shard_map/all_to_all | solution.py:131
  88.6 1.0 copy-done.13
  89.7 1.0 copy-done.15
  91.7 1.4 stage.11
  95.2 3.5 %all-to-all-start.4 = ((bf16[16,64,128]{2,1,0:T(8,128)(2,1)}), bf16[16,64,128]{2,1,0:T(8,128)(2,1)S(1)}, u32[]{:S(2)}, u32[]{:S(2)}) async-start(bf16[16,64,128]{2,1,0:T(8,128)(2,1)} %copy-done.56), calls=%async_computation.4 | async-start | bytes 524288 | tf_op jit(solution)/shard_map/all_to_all | solution.py:131
  98.8 1.6 collective-permute-start.4
  100.4 8.4 %all-to-all-done.4.near = bf16[16,64,128]{2,1,0:T(8,128)(2,1)S(1)} async-done(((bf16[16,64,128]{2,1,0:T(8,128)(2,1)}), bf16[16,64,128]{2,1,0:T(8,128)(2,1)S(1)}, u32[]{:S(2)}, u32[]{:S(2)}) %all-to-all-start.4) | async-done | bytes 262176 | tf_op jit(solution)/shard_map/all_to_all | solution.py:131
  108.8 1.0 copy-done.7
  110.8 1.3 stage.12
  115.1 3.5 %all-to-all-start.5 = ((bf16[16,64,128]{2,1,0:T(8,128)(2,1)}), bf16[16,64,128]{2,1,0:T(8,128)(2,1)S(1)}, u32[]{:S(2)}, u32[]{:S(2)}) async-start(bf16[16,64,128]{2,1,0:T(8,128)(2,1)} %copy-done.58), calls=%async_computation.5 | async-start | bytes 524288 | tf_op jit(solution)/shard_map/all_to_all | solution.py:131
  118.6 1.6 collective-permute-start.5
  120.2 8.4 %all-to-all-done.5.near = bf16[16,64,128]{2,1,0:T(8,128)(2,1)S(1)} async-done(((bf16[16,64,128]{2,1,0:T(8,128)(2,1)}), bf16[16,64,128]{2,1,0:T(8,128)(2,1)S(1)}, u32[]{:S(2)}, u32[]{:S(2)}) %all-to-all-start.5) | async-done | bytes 262176 | tf_op jit(solution)/shard_map/all_to_all | solution.py:131
  128.6 1.0 copy-done.8
  129.7 1.0 copy-done.29
  130.7 1.0 copy-done.31
  132.7 1.3 stage.13
  137.1 3.5 %all-to-all-start.6 = ((bf16[16,64,128]{2,1,0:T(8,128)(2,1)}), bf16[16,64,128]{2,1,0:T(8,128)(2,1)S(1)}, u32[]{:S(2)}, u32[]{:S(2)}) async-start(bf16[16,64,128]{2,1,0:T(8,128)(2,1)} %copy-done.55), calls=%async_computation.6 | async-start | bytes 524288 | tf_op jit(solution)/shard_map/all_to_all | solution.py:131
  140.6 1.6 collective-permute-start.6
  142.2 8.4 %all-to-all-done.6.near = bf16[16,64,128]{2,1,0:T(8,128)(2,1)S(1)} async-done(((bf16[16,64,128]{2,1,0:T(8,128)(2,1)}), bf16[16,64,128]{2,1,0:T(8,128)(2,1)S(1)}, u32[]{:S(2)}, u32[]{:S(2)}) %all-to-all-start.6) | async-done | bytes 262176 | tf_op jit(solution)/shard_map/all_to_all | solution.py:131
  150.6 1.0 copy-done.9
  154.7 1.3 stage.14
  159.0 3.5 %all-to-all-start.7 = ((bf16[16,64,128]{2,1,0:T(8,128)(2,1)}), bf16[16,64,128]{2,1,0:T(8,128)(2,1)S(1)}, u32[]{:S(2)}, u32[]{:S(2)}) async-start(bf16[16,64,128]{2,1,0:T(8,128)(2,1)} %copy-done.52), calls=%async_computation.7 | async-start | bytes 524288 | tf_op jit(solution)/shard_map/all_to_all | solution.py:131
  162.6 1.6 collective-permute-start.7
  164.2 8.4 %all-to-all-done.7.near = bf16[16,64,128]{2,1,0:T(8,128)(2,1)S(1)} async-done(((bf16[16,64,128]{2,1,0:T(8,128)(2,1)}), bf16[16,64,128]{2,1,0:T(8,128)(2,1)S(1)}, u32[]{:S(2)}, u32[]{:S(2)}) %all-to-all-start.7) | async-done | bytes 262176 | tf_op jit(solution)/shard_map/all_to_all | solution.py:131
  172.5 1.0 copy-done.33
  175.6 2.1 %stage.15 = f32[16,64,128]{2,1,0:T(8,128)} custom-call(s32[117]{0:T(128)S(1)} %concatenate.3.table.refs_0_, bf16[16,768,128]{2,1,0:T(8,128)(2,1)S(1)} %bitcast.12, f32[16,128]{1,0:T(8,128)S(1)} %copy-done.11, bf16[16,64,128]{2,1,0:T(8,128)(2,1)S(1)} %copy-done.49, bf16[16,64,128]{2,1,0:T(8,128)(2,1)S(1)} %landed.15.refs_4_, ...), custom_call_target="tpu_custom_call" | custom-call | flops 201326592 | bytes 3145728 | tf_op jit(solution)/shard_map/stage/pallas_call | solution.py:166
  (122 shorter events, 36.2 us)
Async XLA Ops:
  1.6 1.0 copy-start.2
  4.7 40.0 %copy-start.11 = (f32[16,128]{1,0:T(8,128)S(1)}, f32[16,128]{1,0:T(8,128)}, u32[]{:S(2)}) copy-start(f32[16,128]{1,0:T(8,128)} %refs_2_.15) | copy-start | bytes 24580
  4.7 17.5 %all-to-all-start = ((bf16[16,64,128]{2,1,0:T(8,128)(2,1)}), bf16[16,64,128]{2,1,0:T(8,128)(2,1)S(1)}, u32[]{:S(2)}, u32[]{:S(2)}) async-start(bf16[16,64,128]{2,1,0:T(8,128)(2,1)} %get-tuple-element.43), calls=%async_computation | async-start | bytes 524288 | tf_op jit(solution)/shard_map/all_to_all | solution.py:131
  12.2 10.0 %collective-permute-start = (bf16[2,64,128]{2,1,0:T(8,128)(2,1)S(1)}, bf16[2,64,128]{2,1,0:T(8,128)(2,1)S(1)}, u32[]{:S(2)}, u32[]{:S(2)}) collective-permute-start(bf16[2,64,128]{2,1,0:T(8,128)(2,1)S(1)} %get-tuple-element.44), channel_id=1, source_target_pairs={{0,16},{16,0},{1,17},{17,1},{2,18},{18,2},{3,19},{19,3},{4,20},{20... | collective-permute-start | bytes 98312 | tf_op jit(solution)/shard_map/ppermute | solution.py:130
  22.2 1.9 %copy-start = (bf16[16,6,128,128]{3,2,1,0:T(8,128)(2,1)S(1)}, bf16[16,6,128,128]{3,2,1,0:T(8,128)(2,1)}, u32[]{:S(2)}) copy-start(bf16[16,6,128,128]{3,2,1,0:T(8,128)(2,1)} %param.9) | copy-start | bytes 9437188
  24.1 1.0 copy-start.3
  25.9 0.9 copy-start.51
  26.8 17.9 %copy-start.1 = (bf16[16,6,128,128]{3,2,1,0:T(8,128)(2,1)S(1)}, bf16[16,6,128,128]{3,2,1,0:T(8,128)(2,1)}, u32[]{:S(2)}) copy-start(bf16[16,6,128,128]{3,2,1,0:T(8,128)(2,1)} %param.9) | copy-start | bytes 9437188
  31.2 13.5 %all-to-all-start.1 = ((bf16[16,64,128]{2,1,0:T(8,128)(2,1)}), bf16[16,64,128]{2,1,0:T(8,128)(2,1)S(1)}, u32[]{:S(2)}, u32[]{:S(2)}) async-start(bf16[16,64,128]{2,1,0:T(8,128)(2,1)} %copy-done.57), calls=%async_computation.1 | async-start | bytes 524288 | tf_op jit(solution)/shard_map/all_to_all | solution.py:131
  34.7 10.0 %collective-permute-start.1 = (bf16[2,64,128]{2,1,0:T(8,128)(2,1)S(1)}, bf16[2,64,128]{2,1,0:T(8,128)(2,1)S(1)}, u32[]{:S(2)}, u32[]{:S(2)}) collective-permute-start(bf16[2,64,128]{2,1,0:T(8,128)(2,1)S(1)} %get-tuple-element.47), channel_id=1, source_target_pairs={{0,16},{16,0},{1,17},{17,1},{2,18},{18,2},{3,19},{19,3},{4,20},{20... | collective-permute-start | bytes 98312 | tf_op jit(solution)/shard_map/ppermute | solution.py:130
  44.7 1.0 copy-start.4
  45.8 1.0 copy-start.25
  46.8 1.0 copy-start.27
  47.8 0.9 copy-start.45
  53.1 13.5 %all-to-all-start.2 = ((bf16[16,64,128]{2,1,0:T(8,128)(2,1)}), bf16[16,64,128]{2,1,0:T(8,128)(2,1)S(1)}, u32[]{:S(2)}, u32[]{:S(2)}) async-start(bf16[16,64,128]{2,1,0:T(8,128)(2,1)} %copy-done.53), calls=%async_computation.2 | async-start | bytes 524288 | tf_op jit(solution)/shard_map/all_to_all | solution.py:131
  56.7 10.0 %collective-permute-start.2 = (bf16[2,64,128]{2,1,0:T(8,128)(2,1)S(1)}, bf16[2,64,128]{2,1,0:T(8,128)(2,1)S(1)}, u32[]{:S(2)}, u32[]{:S(2)}) collective-permute-start(bf16[2,64,128]{2,1,0:T(8,128)(2,1)S(1)} %get-tuple-element.52), channel_id=1, source_target_pairs={{0,16},{16,0},{1,17},{17,1},{2,18},{18,2},{3,19},{19,3},{4,20},{20... | collective-permute-start | bytes 98312 | tf_op jit(solution)/shard_map/ppermute | solution.py:130
  66.7 1.0 copy-start.5
  67.7 1.0 copy-start.21
  68.8 1.0 copy-start.23
  69.8 0.9 copy-start.39
  75.1 13.5 %all-to-all-start.3 = ((bf16[16,64,128]{2,1,0:T(8,128)(2,1)}), bf16[16,64,128]{2,1,0:T(8,128)(2,1)S(1)}, u32[]{:S(2)}, u32[]{:S(2)}) async-start(bf16[16,64,128]{2,1,0:T(8,128)(2,1)} %copy-done.54), calls=%async_computation.3 | async-start | bytes 524288 | tf_op jit(solution)/shard_map/all_to_all | solution.py:131
  78.6 10.0 %collective-permute-start.3 = (bf16[2,64,128]{2,1,0:T(8,128)(2,1)S(1)}, bf16[2,64,128]{2,1,0:T(8,128)(2,1)S(1)}, u32[]{:S(2)}, u32[]{:S(2)}) collective-permute-start(bf16[2,64,128]{2,1,0:T(8,128)(2,1)S(1)} %get-tuple-element.57), channel_id=1, source_target_pairs={{0,16},{16,0},{1,17},{17,1},{2,18},{18,2},{3,19},{19,3},{4,20},{20... | collective-permute-start | bytes 98312 | tf_op jit(solution)/shard_map/ppermute | solution.py:130
  88.6 1.0 copy-start.13
  89.7 1.0 copy-start.15
  90.7 0.9 copy-start.41
  95.2 13.5 %all-to-all-start.4 = ((bf16[16,64,128]{2,1,0:T(8,128)(2,1)}), bf16[16,64,128]{2,1,0:T(8,128)(2,1)S(1)}, u32[]{:S(2)}, u32[]{:S(2)}) async-start(bf16[16,64,128]{2,1,0:T(8,128)(2,1)} %copy-done.56), calls=%async_computation.4 | async-start | bytes 524288 | tf_op jit(solution)/shard_map/all_to_all | solution.py:131
  98.8 10.0 %collective-permute-start.4 = (bf16[2,64,128]{2,1,0:T(8,128)(2,1)S(1)}, bf16[2,64,128]{2,1,0:T(8,128)(2,1)S(1)}, u32[]{:S(2)}, u32[]{:S(2)}) collective-permute-start(bf16[2,64,128]{2,1,0:T(8,128)(2,1)S(1)} %get-tuple-element.62), channel_id=1, source_target_pairs={{0,16},{16,0},{1,17},{17,1},{2,18},{18,2},{3,19},{19,3},{4,20},{20... | collective-permute-start | bytes 98312 | tf_op jit(solution)/shard_map/ppermute | solution.py:130
  108.8 1.0 copy-start.7
  109.8 0.9 copy-start.43
  112.1 0.8 copy-start.28
  115.1 13.5 %all-to-all-start.5 = ((bf16[16,64,128]{2,1,0:T(8,128)(2,1)}), bf16[16,64,128]{2,1,0:T(8,128)(2,1)S(1)}, u32[]{:S(2)}, u32[]{:S(2)}) async-start(bf16[16,64,128]{2,1,0:T(8,128)(2,1)} %copy-done.58), calls=%async_computation.5 | async-start | bytes 524288 | tf_op jit(solution)/shard_map/all_to_all | solution.py:131
  118.6 10.0 %collective-permute-start.5 = (bf16[2,64,128]{2,1,0:T(8,128)(2,1)S(1)}, bf16[2,64,128]{2,1,0:T(8,128)(2,1)S(1)}, u32[]{:S(2)}, u32[]{:S(2)}) collective-permute-start(bf16[2,64,128]{2,1,0:T(8,128)(2,1)S(1)} %get-tuple-element.66), channel_id=1, source_target_pairs={{0,16},{16,0},{1,17},{17,1},{2,18},{18,2},{3,19},{19,3},{4,20},{20... | collective-permute-start | bytes 98312 | tf_op jit(solution)/shard_map/ppermute | solution.py:130
  128.6 1.0 copy-start.8
  129.7 1.0 copy-start.29
  130.7 1.0 copy-start.31
  131.8 0.9 copy-start.47
  134.0 0.8 copy-start.16
  137.1 13.5 %all-to-all-start.6 = ((bf16[16,64,128]{2,1,0:T(8,128)(2,1)}), bf16[16,64,128]{2,1,0:T(8,128)(2,1)S(1)}, u32[]{:S(2)}, u32[]{:S(2)}) async-start(bf16[16,64,128]{2,1,0:T(8,128)(2,1)} %copy-done.55), calls=%async_computation.6 | async-start | bytes 524288 | tf_op jit(solution)/shard_map/all_to_all | solution.py:131
  140.6 10.0 %collective-permute-start.6 = (bf16[2,64,128]{2,1,0:T(8,128)(2,1)S(1)}, bf16[2,64,128]{2,1,0:T(8,128)(2,1)S(1)}, u32[]{:S(2)}, u32[]{:S(2)}) collective-permute-start(bf16[2,64,128]{2,1,0:T(8,128)(2,1)S(1)} %get-tuple-element.71), channel_id=1, source_target_pairs={{0,16},{16,0},{1,17},{17,1},{2,18},{18,2},{3,19},{19,3},{4,20},{20... | collective-permute-start | bytes 98312 | tf_op jit(solution)/shard_map/ppermute | solution.py:130
  150.6 1.0 copy-start.9
  151.6 1.0 copy-start.17
  152.7 1.0 copy-start.19
  153.7 0.9 copy-start.37
  159.0 13.5 %all-to-all-start.7 = ((bf16[16,64,128]{2,1,0:T(8,128)(2,1)}), bf16[16,64,128]{2,1,0:T(8,128)(2,1)S(1)}, u32[]{:S(2)}, u32[]{:S(2)}) async-start(bf16[16,64,128]{2,1,0:T(8,128)(2,1)} %copy-done.52), calls=%async_computation.7 | async-start | bytes 524288 | tf_op jit(solution)/shard_map/all_to_all | solution.py:131
  162.6 10.0 %collective-permute-start.7 = (bf16[2,64,128]{2,1,0:T(8,128)(2,1)S(1)}, bf16[2,64,128]{2,1,0:T(8,128)(2,1)S(1)}, u32[]{:S(2)}, u32[]{:S(2)}) collective-permute-start(bf16[2,64,128]{2,1,0:T(8,128)(2,1)S(1)} %get-tuple-element.76), channel_id=1, source_target_pairs={{0,16},{16,0},{1,17},{17,1},{2,18},{18,2},{3,19},{19,3},{4,20},{20... | collective-permute-start | bytes 98312 | tf_op jit(solution)/shard_map/ppermute | solution.py:130
  172.5 1.0 copy-start.33
  173.6 1.0 copy-start.35
  174.6 0.9 copy-start.49
  (27 other events, 20.2 us)

commit v3 on v2

--- a/solution.py
+++ b/solution.py
@@ -9,7 +9,6 @@
 
 
 STEPS = 2
-PIECES = 1
 
 
 step_size = 0.1
@@ -28,7 +27,6 @@
         self.near = member_col.shape[1]
         self.far = group_col.shape[1]
         self.sent = group_send.shape[1] // self.groups
-        self.piece = self.traj // PIECES
         self.at_own = 0
         self.at_near = self.at_own + self.rows
         self.at_far = self.at_near + self.rows * self.near
@@ -38,26 +36,52 @@
 
 
 def group_row(sz, table, shift, slot):
-    target = lax.rem(table[sz.at_group] + shift, sz.groups)
-    return table[sz.at_gsend + target * sz.sent + slot]
+    target = lax.rem(table[0, sz.at_group] + shift, sz.groups)
+    return table[0, sz.at_gsend + target * sz.sent + slot]
 
 
 def fill_sends(sz, table, rounded, member_out, group_out):
     for p in range(sz.members):
-        member_out[p] = rounded[table[sz.at_msend + p]]
+        member_out[p] = rounded[table[0, sz.at_msend + p]]
     for shift in range(1, sz.groups):
         for slot in range(sz.sent):
             group_out[(shift - 1) * sz.sent + slot] = rounded[group_row(sz, table, shift, slot)]
 
 
-def first_kernel(sz, piece, table, state, rounded, member_out, group_out):
-    span = pl.ds(piece * sz.piece, sz.piece)
+def first_kernel(sz, own_col, near_col, far_col, member_send, group_send, state_far, blocks_far, rate_far,
+                 table_out, state, blocks, rate, rounded, member_out, group_out, table, sems):
+    copies = [
+        pltpu.make_async_copy(state_far, state, sems.at[0]),
+        pltpu.make_async_copy(rate_far, rate, sems.at[1]),
+        pltpu.make_async_copy(blocks_far, blocks, sems.at[2]),
+    ]
+    for copy in copies:
+        copy.start()
     for i in range(sz.rows):
-        rounded[i] = state[i, span].astype(jnp.bfloat16)
+        table[0, sz.at_own + i] = own_col[i]
+        for k in range(sz.near):
+            table[0, sz.at_near + i * sz.near + k] = near_col[k, i]
+        for k in range(sz.far):
+            table[0, sz.at_far + i * sz.far + k] = far_col[k, i]
+    for p in range(sz.members):
+        table[0, sz.at_msend + p] = member_send[0, p]
+    for slot in range(sz.groups * sz.sent):
+        table[0, sz.at_gsend + slot] = group_send[0, slot]
+    table[0, sz.at_group] = lax.axis_index("group")
+    for i in range(sz.at_group + 1, table.shape[1]):
+        table[0, i] = 0
+    keep = pltpu.make_async_copy(table, table_out, sems.at[3])
+    keep.start()
+    copies[0].wait()
+    for i in range(sz.rows):
+        rounded[i] = state[i].astype(jnp.bfloat16)
     fill_sends(sz, table, rounded, member_out, group_out)
-
-
-def stage_kernel(sz, stage, last, base_span, *refs):
+    keep.wait()
+    copies[1].wait()
+    copies[2].wait()
+
+
+def stage_kernel(sz, stage, last, *refs):
     it = iter(refs)
     table, blocks, rate, rounded, near, far = (next(it) for _ in range(6))
     base = next(it) if stage < 3 else None
@@ -74,18 +98,18 @@
     for j in range((sz.groups - 1) * sz.sent):
         far_all[sz.sent + j] = far[j]
 
-    group = table[sz.at_group]
+    group = table[0, sz.at_group]
     for i in range(sz.rows):
-        parts = [rounded[table[sz.at_own + i]]]
+        parts = [rounded[table[0, sz.at_own + i]]]
         for k in range(sz.near):
-            parts.append(near[table[sz.at_near + i * sz.near + k]])
+            parts.append(near[table[0, sz.at_near + i * sz.near + k]])
         for k in range(sz.far):
-            col = table[sz.at_far + i * sz.far + k]
+            col = table[0, sz.at_far + i * sz.far + k]
             place = lax.rem(group + sz.groups - lax.div(col, sz.sent), sz.groups)
             parts.append(far_all[place * sz.sent + lax.rem(col, sz.sent)])
         left = jnp.concatenate(parts, axis=1)
         product = jnp.dot(left, blocks[i], preferred_element_type=jnp.float32)
-        start = base[i, base_span] if stage < 3 else None
+        start = base[i] if stage < 3 else None
         v = start if stage == 0 else value[i]
         slope = rate[i : i + 1] * (v - v * v * v) - product
         if stage < 3:
@@ -105,22 +129,15 @@
 def solution(mesh):
     def per_device(state, blocks, rate, own_col, member_col, group_col, member_send, group_send):
         sz = Sizes(mesh, state, member_col, group_col, group_send)
-        table = jnp.concatenate(
-            [
-                own_col.reshape(-1),
-                member_col.reshape(-1),
-                group_col.reshape(-1),
-                member_send.reshape(-1),
-                group_send.reshape(-1),
-                lax.axis_index("group").astype(jnp.int32).reshape(1),
-            ]
-        )
-        weights = blocks.reshape(sz.rows, -1, sz.cells)
-        f32 = jax.ShapeDtypeStruct((sz.rows, sz.piece, sz.cells), jnp.float32)
-        bf16 = lambda n: jax.ShapeDtypeStruct((n, sz.piece, sz.cells), jnp.bfloat16)
+        far_off = lambda x: pltpu.with_memory_space_constraint(x, pltpu.MemorySpace.HBM)
+        held = lambda x: pltpu.VMEM(x.shape, x.dtype)
+        weights = far_off(blocks.reshape(sz.rows, -1, sz.cells))
+        entries = -(-(sz.at_group + 1) // 128) * 128
+        f32 = jax.ShapeDtypeStruct((sz.rows, sz.traj, sz.cells), jnp.float32)
+        bf16 = lambda n: jax.ShapeDtypeStruct((n, sz.traj, sz.cells), jnp.bfloat16)
         sends = [bf16(sz.rows), bf16(sz.members), bf16((sz.groups - 1) * sz.sent)]
         limit = 16 * 2**20
-        flops = 2 * sz.rows * weights.shape[1] * sz.cells * sz.piece
+        flops = 2 * sz.rows * weights.shape[1] * sz.cells * sz.traj
 
         def exchange(member_out, group_out):
             far = []
@@ -143,32 +160,32 @@
                 name="landed",
             )(near)
 
-        def begin(piece):
+        def begin():
+            tables = [own_col, member_col.T, group_col.T, member_send, group_send]
             return pl.pallas_call(
-                functools.partial(first_kernel, sz, piece),
-                out_shape=sends,
-                in_specs=[SMEM, VMEM],
-                out_specs=[VMEM] * 3,
+                functools.partial(first_kernel, sz),
+                out_shape=[pltpu.VMEM((1, entries), jnp.int32), held(state), held(weights), held(rate), *sends],
+                in_specs=[SMEM] * 5 + [ANY] * 3,
+                out_specs=[VMEM] * 7,
+                scratch_shapes=[pltpu.SMEM((1, entries), jnp.int32), pltpu.SemaphoreType.DMA((4,))],
                 compiler_params=pltpu.CompilerParams(vmem_limit_bytes=limit),
                 name="begin",
-            )(table, state)
-
-        def advance(stage, last, piece, carry, near, far):
+            )(*map(far_off, tables), far_off(state), weights, far_off(rate))
+
+        def advance(stage, last, carry, near, far):
             rounded, base, value, total = carry
-            whole = base.shape[1] == sz.traj
-            span = pl.ds(piece * sz.piece if whole else 0, sz.piece)
-            ops = [table, weights, rate, rounded, near, far]
+            ops = [table, held_weights, held_rate, rounded, near, far]
             if stage < 3:
                 ops.append(base)
             if stage > 0:
                 ops += [value, total]
             outs = ([] if last else list(sends)) + [f32] + ([f32] if stage < 3 else [])
             got = pl.pallas_call(
-                functools.partial(stage_kernel, sz, stage, last, span),
+                functools.partial(stage_kernel, sz, stage, last),
                 out_shape=outs,
                 in_specs=[SMEM] + [VMEM] * (len(ops) - 1),
                 out_specs=[VMEM] * len(outs),
-                scratch_shapes=[pltpu.VMEM((sz.groups * sz.sent, sz.piece, sz.cells), jnp.bfloat16)],
+                scratch_shapes=[pltpu.VMEM((sz.groups * sz.sent, sz.traj, sz.cells), jnp.bfloat16)],
                 compiler_params=pltpu.CompilerParams(vmem_limit_bytes=limit),
                 cost_estimate=pl.CostEstimate(flops=flops, bytes_accessed=weights.size * 2, transcendentals=0),
                 name="stage",
@@ -179,20 +196,14 @@
                 return (got[0], base, got[3], got[4]), got[1], got[2]
             return (got[0], got[3], None, None), got[1], got[2]
 
-        carries, outgoing = [], []
-        for piece in range(PIECES):
-            rounded, member_out, group_out = begin(piece)
-            carries.append((rounded, state, None, None))
-            outgoing.append((member_out, group_out))
+        table, base, held_weights, held_rate, rounded, member_out, group_out = begin()
+        carry = (rounded, base, None, None)
         for step in range(STEPS):
             for stage in range(4):
                 last = step == STEPS - 1 and stage == 3
-                for piece in range(PIECES):
-                    near, far = exchange(*outgoing[piece])
-                    carry, member_out, group_out = advance(stage, last, piece, carries[piece], near, far)
-                    carries[piece] = carry
-                    outgoing[piece] = (member_out, group_out)
-        return carries[0] if PIECES == 1 else jnp.concatenate(carries, axis=1)
+                near, far = exchange(member_out, group_out)
+                carry, member_out, group_out = advance(stage, last, carry, near, far)
+        return carry
 
     return jax.shard_map(
         per_device,

time: 180 us -> 177 us (0.983)
  local copies, waits for them, and re-layouts: 52.6 us -> 48.7 us
    unnamed x119 -> x112, local copies, waits for them, and re-layouts: 51.8 us -> 48.7 us
where the time goes in v3:
time: 177 us; the launch traced here: 175 us
  waiting for transfers between devices  67.2 us (38%)
  local copies, waits for them, and re-layouts  48.7 us (28%)
  starting transfers between devices  44.7 us (25%)
  Pallas kernels  14.4 us (8%)
    all_to_all x8, waiting for transfers between devices, exchange(): lax.all_to_all(member_out, 'member', split_axis=0, concat_axis=0, tiled=T...  67.2 us
    unnamed x112, local copies, waits for them, and re-layouts  48.7 us
    all_to_all x8, starting transfers between devices, exchange(): lax.all_to_all(member_out, 'member', split_axis=0, concat_axis=0, tiled=T...  32.1 us
    ppermute x8, starting transfers between devices, exchange(): far.append(lax.ppermute(sent, 'group', pairs))  12.6 us
    pallas_call x8, Pallas kernels, advance(): pl.pallas_call(functools.partial(stage_kernel, sz, stage, last), out_shap...  11.5 us
  transfers between devices with their start and end apart: 16, of which 8 were waited for; matrix products, arithmetic and copies ran while one was open for 0% of the time, Pallas kernels for 0%

profile of v3, /device:TPU:0, one launch (start us, length us, event | category | flops | bytes accessed | tf_op | source)
XLA Modules:
  0.0 175.3 jit_solution(2857586277282126196)
XLA Ops:
  0.0 2.8 %begin.1 = (s32[1,128]{1,0:T(1,128)S(1)}, f32[16,64,128]{2,1,0:T(8,128)S(1)}, bf16[16,768,128]{2,1,0:T(8,128)(2,1)S(1)}, f32[16,128]{1,0:T(8,128)S(1)}, bf16[16,...) custom-call(s32[16]{0:T(128)} %own_col.1, s32[4,16]{1,0:T(4,128)} %bitcast.4, ...), custom_call_target="tpu_custom_call" | custom-call | tf_op jit(solution)/shard_map/begin/pallas_call | solution.py:165
  5.0 7.4 %all-to-all-start = ((bf16[16,64,128]{2,1,0:T(8,128)(2,1)}), bf16[16,64,128]{2,1,0:T(8,128)(2,1)S(1)}, u32[]{:S(2)}, u32[]{:S(2)}) async-start(bf16[16,64,128]{2,1,0:T(8,128)(2,1)} %copy-done.55), calls=%async_computation | async-start | bytes 524288 | tf_op jit(solution)/shard_map/all_to_all | solution.py:148
  12.4 1.6 collective-permute-start
  14.0 8.4 %all-to-all-done.near = bf16[16,64,128]{2,1,0:T(8,128)(2,1)S(1)} async-done(((bf16[16,64,128]{2,1,0:T(8,128)(2,1)}), bf16[16,64,128]{2,1,0:T(8,128)(2,1)S(1)}, u32[]{:S(2)}, u32[]{:S(2)}) %all-to-all-start) | async-done | bytes 262176 | tf_op jit(solution)/shard_map/all_to_all | solution.py:148
  22.4 1.0 copy-done.5
  24.4 1.3 stage.8
  28.8 3.5 %all-to-all-start.1 = ((bf16[16,64,128]{2,1,0:T(8,128)(2,1)}), bf16[16,64,128]{2,1,0:T(8,128)(2,1)S(1)}, u32[]{:S(2)}, u32[]{:S(2)}) async-start(bf16[16,64,128]{2,1,0:T(8,128)(2,1)} %copy-done.53), calls=%async_computation.1 | async-start | bytes 524288 | tf_op jit(solution)/shard_map/all_to_all | solution.py:148
  32.3 1.6 collective-permute-start.1
  33.9 8.4 %all-to-all-done.1.near = bf16[16,64,128]{2,1,0:T(8,128)(2,1)S(1)} async-done(((bf16[16,64,128]{2,1,0:T(8,128)(2,1)}), bf16[16,64,128]{2,1,0:T(8,128)(2,1)S(1)}, u32[]{:S(2)}, u32[]{:S(2)}) %all-to-all-start.1) | async-done | bytes 262176 | tf_op jit(solution)/shard_map/all_to_all | solution.py:148
  42.3 1.0 copy-done.6
  43.4 1.0 copy-done.25
  44.4 1.0 copy-done.27
  46.4 1.3 stage.9
  50.8 3.5 %all-to-all-start.2 = ((bf16[16,64,128]{2,1,0:T(8,128)(2,1)}), bf16[16,64,128]{2,1,0:T(8,128)(2,1)S(1)}, u32[]{:S(2)}, u32[]{:S(2)}) async-start(bf16[16,64,128]{2,1,0:T(8,128)(2,1)} %copy-done.50), calls=%async_computation.2 | async-start | bytes 524288 | tf_op jit(solution)/shard_map/all_to_all | solution.py:148
  54.3 1.6 collective-permute-start.2
  55.9 8.4 %all-to-all-done.2.near = bf16[16,64,128]{2,1,0:T(8,128)(2,1)S(1)} async-done(((bf16[16,64,128]{2,1,0:T(8,128)(2,1)}), bf16[16,64,128]{2,1,0:T(8,128)(2,1)S(1)}, u32[]{:S(2)}, u32[]{:S(2)}) %all-to-all-start.2) | async-done | bytes 262176 | tf_op jit(solution)/shard_map/all_to_all | solution.py:148
  64.3 1.0 copy-done.7
  65.3 1.0 copy-done.13
  66.4 1.0 copy-done.15
  68.4 1.3 stage.10
  72.7 3.5 %all-to-all-start.3 = ((bf16[16,64,128]{2,1,0:T(8,128)(2,1)}), bf16[16,64,128]{2,1,0:T(8,128)(2,1)S(1)}, u32[]{:S(2)}, u32[]{:S(2)}) async-start(bf16[16,64,128]{2,1,0:T(8,128)(2,1)} %copy-done.48), calls=%async_computation.3 | async-start | bytes 524288 | tf_op jit(solution)/shard_map/all_to_all | solution.py:148
  76.2 1.6 collective-permute-start.3
  77.8 8.4 %all-to-all-done.3.near = bf16[16,64,128]{2,1,0:T(8,128)(2,1)S(1)} async-done(((bf16[16,64,128]{2,1,0:T(8,128)(2,1)}), bf16[16,64,128]{2,1,0:T(8,128)(2,1)S(1)}, u32[]{:S(2)}, u32[]{:S(2)}) %all-to-all-start.3) | async-done | bytes 262176 | tf_op jit(solution)/shard_map/all_to_all | solution.py:148
  86.2 1.0 copy-done.9
  87.3 1.0 copy-done.11
  89.3 1.3 stage.11
  92.8 3.5 %all-to-all-start.4 = ((bf16[16,64,128]{2,1,0:T(8,128)(2,1)}), bf16[16,64,128]{2,1,0:T(8,128)(2,1)S(1)}, u32[]{:S(2)}, u32[]{:S(2)}) async-start(bf16[16,64,128]{2,1,0:T(8,128)(2,1)} %copy-done.52), calls=%async_computation.4 | async-start | bytes 524288 | tf_op jit(solution)/shard_map/all_to_all | solution.py:148
  96.3 1.6 collective-permute-start.4
  97.9 8.4 %all-to-all-done.4.near = bf16[16,64,128]{2,1,0:T(8,128)(2,1)S(1)} async-done(((bf16[16,64,128]{2,1,0:T(8,128)(2,1)}), bf16[16,64,128]{2,1,0:T(8,128)(2,1)S(1)}, u32[]{:S(2)}, u32[]{:S(2)}) %all-to-all-start.4) | async-done | bytes 262176 | tf_op jit(solution)/shard_map/all_to_all | solution.py:148
  106.3 1.0 copy-done.1
  108.3 1.3 stage.12
  112.7 3.5 %all-to-all-start.5 = ((bf16[16,64,128]{2,1,0:T(8,128)(2,1)}), bf16[16,64,128]{2,1,0:T(8,128)(2,1)S(1)}, u32[]{:S(2)}, u32[]{:S(2)}) async-start(bf16[16,64,128]{2,1,0:T(8,128)(2,1)} %copy-done.54), calls=%async_computation.5 | async-start | bytes 524288 | tf_op jit(solution)/shard_map/all_to_all | solution.py:148
  116.2 1.6 collective-permute-start.5
  117.8 8.4 %all-to-all-done.5.near = bf16[16,64,128]{2,1,0:T(8,128)(2,1)S(1)} async-done(((bf16[16,64,128]{2,1,0:T(8,128)(2,1)}), bf16[16,64,128]{2,1,0:T(8,128)(2,1)S(1)}, u32[]{:S(2)}, u32[]{:S(2)}) %all-to-all-start.5) | async-done | bytes 262176 | tf_op jit(solution)/shard_map/all_to_all | solution.py:148
  126.2 1.0 copy-done.2
  127.3 1.0 copy-done.29
  130.3 1.3 stage.13
  134.7 3.5 %all-to-all-start.6 = ((bf16[16,64,128]{2,1,0:T(8,128)(2,1)}), bf16[16,64,128]{2,1,0:T(8,128)(2,1)S(1)}, u32[]{:S(2)}, u32[]{:S(2)}) async-start(bf16[16,64,128]{2,1,0:T(8,128)(2,1)} %copy-done.51), calls=%async_computation.6 | async-start | bytes 524288 | tf_op jit(solution)/shard_map/all_to_all | solution.py:148
  138.2 1.6 collective-permute-start.6
  139.8 8.4 %all-to-all-done.6.near = bf16[16,64,128]{2,1,0:T(8,128)(2,1)S(1)} async-done(((bf16[16,64,128]{2,1,0:T(8,128)(2,1)}), bf16[16,64,128]{2,1,0:T(8,128)(2,1)S(1)}, u32[]{:S(2)}, u32[]{:S(2)}) %all-to-all-start.6) | async-done | bytes 262176 | tf_op jit(solution)/shard_map/all_to_all | solution.py:148
  148.2 1.0 copy-done.3
  149.2 1.0 copy-done.17
  152.3 1.3 stage.14
  156.6 3.5 %all-to-all-start.7 = ((bf16[16,64,128]{2,1,0:T(8,128)(2,1)}), bf16[16,64,128]{2,1,0:T(8,128)(2,1)S(1)}, u32[]{:S(2)}, u32[]{:S(2)}) async-start(bf16[16,64,128]{2,1,0:T(8,128)(2,1)} %copy-done.49), calls=%async_computation.7 | async-start | bytes 524288 | tf_op jit(solution)/shard_map/all_to_all | solution.py:148
  160.1 1.6 collective-permute-start.7
  161.7 8.4 %all-to-all-done.7.near = bf16[16,64,128]{2,1,0:T(8,128)(2,1)S(1)} async-done(((bf16[16,64,128]{2,1,0:T(8,128)(2,1)}), bf16[16,64,128]{2,1,0:T(8,128)(2,1)S(1)}, u32[]{:S(2)}, u32[]{:S(2)}) %all-to-all-start.7) | async-done | bytes 262176 | tf_op jit(solution)/shard_map/all_to_all | solution.py:148
  170.1 1.0 copy-done.21
  173.2 2.1 %stage.15 = f32[16,64,128]{2,1,0:T(8,128)} custom-call(s32[1,128]{1,0:T(1,128)S(1)} %get-tuple-element.46.refs_0_, bf16[16,768,128]{2,1,0:T(8,128)(2,1)S(1)} %get-tuple-element.47.refs_1_, f32[16,128]{1,0:T(8,128)S(1)} %get-tuple-element.48.refs_2_, bf16[16,64,128]{2,1,0:T(8,128)(2,1)S(1)} %copy-done.41, bf16[16,64,128]{2,1,0:T(8,128)(2,1)S(1)} %landed.15.refs_4_, ...), custom_call_target="tpu_custom_call" | custom-call | flops 201326592 | bytes 3145728 | tf_op jit(solution)/shard_map/stage/pallas_call | solution.py:183
  (113 shorter events, 33.1 us)
Async XLA Ops:
  5.0 17.4 %all-to-all-start = ((bf16[16,64,128]{2,1,0:T(8,128)(2,1)}), bf16[16,64,128]{2,1,0:T(8,128)(2,1)S(1)}, u32[]{:S(2)}, u32[]{:S(2)}) async-start(bf16[16,64,128]{2,1,0:T(8,128)(2,1)} %copy-done.55), calls=%async_computation | async-start | bytes 524288 | tf_op jit(solution)/shard_map/all_to_all | solution.py:148
  12.4 10.0 %collective-permute-start = (bf16[2,64,128]{2,1,0:T(8,128)(2,1)S(1)}, bf16[2,64,128]{2,1,0:T(8,128)(2,1)S(1)}, u32[]{:S(2)}, u32[]{:S(2)}) collective-permute-start(bf16[2,64,128]{2,1,0:T(8,128)(2,1)S(1)} %get-tuple-element.51), channel_id=1, source_target_pairs={{0,16},{16,0},{1,17},{17,1},{2,18},{18,2},{3,19},{19,3},{4,20},{20... | collective-permute-start | bytes 98312 | tf_op jit(solution)/shard_map/ppermute | solution.py:147
  22.4 1.0 copy-start.5
  23.5 0.9 copy-start.47
  25.8 0.8 copy-start.24
  26.6 0.8 copy-start.26
  28.8 13.5 %all-to-all-start.1 = ((bf16[16,64,128]{2,1,0:T(8,128)(2,1)}), bf16[16,64,128]{2,1,0:T(8,128)(2,1)S(1)}, u32[]{:S(2)}, u32[]{:S(2)}) async-start(bf16[16,64,128]{2,1,0:T(8,128)(2,1)} %copy-done.53), calls=%async_computation.1 | async-start | bytes 524288 | tf_op jit(solution)/shard_map/all_to_all | solution.py:148
  32.3 10.0 %collective-permute-start.1 = (bf16[2,64,128]{2,1,0:T(8,128)(2,1)S(1)}, bf16[2,64,128]{2,1,0:T(8,128)(2,1)S(1)}, u32[]{:S(2)}, u32[]{:S(2)}) collective-permute-start(bf16[2,64,128]{2,1,0:T(8,128)(2,1)S(1)} %get-tuple-element.55), channel_id=1, source_target_pairs={{0,16},{16,0},{1,17},{17,1},{2,18},{18,2},{3,19},{19,3},{4,20},{20... | collective-permute-start | bytes 98312 | tf_op jit(solution)/shard_map/ppermute | solution.py:147
  42.3 1.0 copy-start.6
  43.4 1.0 copy-start.25
  44.4 1.0 copy-start.27
  45.5 0.9 copy-start.43
  47.8 0.8 copy-start.12
  48.6 0.8 copy-start.14
  50.8 13.5 %all-to-all-start.2 = ((bf16[16,64,128]{2,1,0:T(8,128)(2,1)}), bf16[16,64,128]{2,1,0:T(8,128)(2,1)S(1)}, u32[]{:S(2)}, u32[]{:S(2)}) async-start(bf16[16,64,128]{2,1,0:T(8,128)(2,1)} %copy-done.50), calls=%async_computation.2 | async-start | bytes 524288 | tf_op jit(solution)/shard_map/all_to_all | solution.py:148
  54.3 10.0 %collective-permute-start.2 = (bf16[2,64,128]{2,1,0:T(8,128)(2,1)S(1)}, bf16[2,64,128]{2,1,0:T(8,128)(2,1)S(1)}, u32[]{:S(2)}, u32[]{:S(2)}) collective-permute-start(bf16[2,64,128]{2,1,0:T(8,128)(2,1)S(1)} %get-tuple-element.60), channel_id=1, source_target_pairs={{0,16},{16,0},{1,17},{17,1},{2,18},{18,2},{3,19},{19,3},{4,20},{20... | collective-permute-start | bytes 98312 | tf_op jit(solution)/shard_map/ppermute | solution.py:147
  64.3 1.0 copy-start.7
  65.3 1.0 copy-start.13
  66.4 1.0 copy-start.15
  67.4 0.9 copy-start.33
  72.7 13.5 %all-to-all-start.3 = ((bf16[16,64,128]{2,1,0:T(8,128)(2,1)}), bf16[16,64,128]{2,1,0:T(8,128)(2,1)S(1)}, u32[]{:S(2)}, u32[]{:S(2)}) async-start(bf16[16,64,128]{2,1,0:T(8,128)(2,1)} %copy-done.48), calls=%async_computation.3 | async-start | bytes 524288 | tf_op jit(solution)/shard_map/all_to_all | solution.py:148
  76.2 10.0 %collective-permute-start.3 = (bf16[2,64,128]{2,1,0:T(8,128)(2,1)S(1)}, bf16[2,64,128]{2,1,0:T(8,128)(2,1)S(1)}, u32[]{:S(2)}, u32[]{:S(2)}) collective-permute-start(bf16[2,64,128]{2,1,0:T(8,128)(2,1)S(1)} %get-tuple-element.65), channel_id=1, source_target_pairs={{0,16},{16,0},{1,17},{17,1},{2,18},{18,2},{3,19},{19,3},{4,20},{20... | collective-permute-start | bytes 98312 | tf_op jit(solution)/shard_map/ppermute | solution.py:147
  86.2 1.0 copy-start.9
  87.3 1.0 copy-start.11
  88.3 0.9 copy-start.37
  92.8 13.5 %all-to-all-start.4 = ((bf16[16,64,128]{2,1,0:T(8,128)(2,1)}), bf16[16,64,128]{2,1,0:T(8,128)(2,1)S(1)}, u32[]{:S(2)}, u32[]{:S(2)}) async-start(bf16[16,64,128]{2,1,0:T(8,128)(2,1)} %copy-done.52), calls=%async_computation.4 | async-start | bytes 524288 | tf_op jit(solution)/shard_map/all_to_all | solution.py:148
  96.3 10.0 %collective-permute-start.4 = (bf16[2,64,128]{2,1,0:T(8,128)(2,1)S(1)}, bf16[2,64,128]{2,1,0:T(8,128)(2,1)S(1)}, u32[]{:S(2)}, u32[]{:S(2)}) collective-permute-start(bf16[2,64,128]{2,1,0:T(8,128)(2,1)S(1)} %get-tuple-element.70), channel_id=1, source_target_pairs={{0,16},{16,0},{1,17},{17,1},{2,18},{18,2},{3,19},{19,3},{4,20},{20... | collective-permute-start | bytes 98312 | tf_op jit(solution)/shard_map/ppermute | solution.py:147
  106.3 1.0 copy-start.1
  107.4 0.9 copy-start.39
  110.5 0.8 copy-start.30
  112.7 13.5 %all-to-all-start.5 = ((bf16[16,64,128]{2,1,0:T(8,128)(2,1)}), bf16[16,64,128]{2,1,0:T(8,128)(2,1)S(1)}, u32[]{:S(2)}, u32[]{:S(2)}) async-start(bf16[16,64,128]{2,1,0:T(8,128)(2,1)} %copy-done.54), calls=%async_computation.5 | async-start | bytes 524288 | tf_op jit(solution)/shard_map/all_to_all | solution.py:148
  116.2 10.0 %collective-permute-start.5 = (bf16[2,64,128]{2,1,0:T(8,128)(2,1)S(1)}, bf16[2,64,128]{2,1,0:T(8,128)(2,1)S(1)}, u32[]{:S(2)}, u32[]{:S(2)}) collective-permute-start(bf16[2,64,128]{2,1,0:T(8,128)(2,1)S(1)} %get-tuple-element.74), channel_id=1, source_target_pairs={{0,16},{16,0},{1,17},{17,1},{2,18},{18,2},{3,19},{19,3},{4,20},{20... | collective-permute-start | bytes 98312 | tf_op jit(solution)/shard_map/ppermute | solution.py:147
  126.2 1.0 copy-start.2
  127.3 1.0 copy-start.29
  128.3 1.0 copy-start.31
  129.3 0.9 copy-start.45
  132.4 0.8 copy-start.18
  134.7 13.5 %all-to-all-start.6 = ((bf16[16,64,128]{2,1,0:T(8,128)(2,1)}), bf16[16,64,128]{2,1,0:T(8,128)(2,1)S(1)}, u32[]{:S(2)}, u32[]{:S(2)}) async-start(bf16[16,64,128]{2,1,0:T(8,128)(2,1)} %copy-done.51), calls=%async_computation.6 | async-start | bytes 524288 | tf_op jit(solution)/shard_map/all_to_all | solution.py:148
  138.2 10.0 %collective-permute-start.6 = (bf16[2,64,128]{2,1,0:T(8,128)(2,1)S(1)}, bf16[2,64,128]{2,1,0:T(8,128)(2,1)S(1)}, u32[]{:S(2)}, u32[]{:S(2)}) collective-permute-start(bf16[2,64,128]{2,1,0:T(8,128)(2,1)S(1)} %get-tuple-element.79), channel_id=1, source_target_pairs={{0,16},{16,0},{1,17},{17,1},{2,18},{18,2},{3,19},{19,3},{4,20},{20... | collective-permute-start | bytes 98312 | tf_op jit(solution)/shard_map/ppermute | solution.py:147
  148.2 1.0 copy-start.3
  149.2 1.0 copy-start.17
  150.3 1.0 copy-start.19
  151.3 0.9 copy-start.35
  156.6 13.5 %all-to-all-start.7 = ((bf16[16,64,128]{2,1,0:T(8,128)(2,1)}), bf16[16,64,128]{2,1,0:T(8,128)(2,1)S(1)}, u32[]{:S(2)}, u32[]{:S(2)}) async-start(bf16[16,64,128]{2,1,0:T(8,128)(2,1)} %copy-done.49), calls=%async_computation.7 | async-start | bytes 524288 | tf_op jit(solution)/shard_map/all_to_all | solution.py:148
  160.1 10.0 %collective-permute-start.7 = (bf16[2,64,128]{2,1,0:T(8,128)(2,1)S(1)}, bf16[2,64,128]{2,1,0:T(8,128)(2,1)S(1)}, u32[]{:S(2)}, u32[]{:S(2)}) collective-permute-start(bf16[2,64,128]{2,1,0:T(8,128)(2,1)S(1)} %get-tuple-element.84), channel_id=1, source_target_pairs={{0,16},{16,0},{1,17},{17,1},{2,18},{18,2},{3,19},{19,3},{4,20},{20... | collective-permute-start | bytes 98312 | tf_op jit(solution)/shard_map/ppermute | solution.py:147
  170.1 1.0 copy-start.21
  171.2 1.0 copy-start.23
  172.2 0.9 copy-start.41
  (24 other events, 17.6 us)

commit v4 on v3

--- a/solution.py
+++ b/solution.py
@@ -48,15 +48,21 @@
             group_out[(shift - 1) * sz.sent + slot] = rounded[group_row(sz, table, shift, slot)]
 
 
-def first_kernel(sz, own_col, near_col, far_col, member_send, group_send, state_far, blocks_far, rate_far,
-                 table_out, state, blocks, rate, rounded, member_out, group_out, table, sems):
+def first_kernel(sz, *refs):
+    indices_far, (state_far, blocks_far, rate_far), refs = refs[:5], refs[5:8], refs[8:]
+    (table, state, blocks, rate, rounded, member_out, group_out), refs = refs[:7], refs[7:]
+    indices, sems = refs[:5], refs[5]
+    own_col, near_col, far_col, member_send, group_send = indices
     copies = [
-        pltpu.make_async_copy(state_far, state, sems.at[0]),
-        pltpu.make_async_copy(rate_far, rate, sems.at[1]),
-        pltpu.make_async_copy(blocks_far, blocks, sems.at[2]),
+        pltpu.make_async_copy(source, target, sems.at[n])
+        for n, (source, target) in enumerate(
+            zip((state_far, rate_far, *indices_far, blocks_far), (state, rate, *indices, blocks))
+        )
     ]
     for copy in copies:
         copy.start()
+    for copy in copies[2:7]:
+        copy.wait()
     for i in range(sz.rows):
         table[0, sz.at_own + i] = own_col[i]
         for k in range(sz.near):
@@ -70,15 +76,12 @@
     table[0, sz.at_group] = lax.axis_index("group")
     for i in range(sz.at_group + 1, table.shape[1]):
         table[0, i] = 0
-    keep = pltpu.make_async_copy(table, table_out, sems.at[3])
-    keep.start()
     copies[0].wait()
     for i in range(sz.rows):
         rounded[i] = state[i].astype(jnp.bfloat16)
     fill_sends(sz, table, rounded, member_out, group_out)
-    keep.wait()
     copies[1].wait()
-    copies[2].wait()
+    copies[7].wait()
 
 
 def stage_kernel(sz, stage, last, *refs):
@@ -164,10 +167,10 @@
             tables = [own_col, member_col.T, group_col.T, member_send, group_send]
             return pl.pallas_call(
                 functools.partial(first_kernel, sz),
-                out_shape=[pltpu.VMEM((1, entries), jnp.int32), held(state), held(weights), held(rate), *sends],
-                in_specs=[SMEM] * 5 + [ANY] * 3,
-                out_specs=[VMEM] * 7,
-                scratch_shapes=[pltpu.SMEM((1, entries), jnp.int32), pltpu.SemaphoreType.DMA((4,))],
+                out_shape=[pltpu.SMEM((1, entries), jnp.int32), held(state), held(weights), held(rate), *sends],
+                in_specs=[ANY] * 8,
+                out_specs=[SMEM] + [VMEM] * 6,
+                scratch_shapes=[pltpu.SMEM(x.shape, x.dtype) for x in tables] + [pltpu.SemaphoreType.DMA((8,))],
                 compiler_params=pltpu.CompilerParams(vmem_limit_bytes=limit),
                 name="begin",
             )(*map(far_off, tables), far_off(state), weights, far_off(rate))

time: 177 us -> 172 us (0.972)
  Pallas kernels: 14.4 us -> 9.29 us
    pallas_call x8, Pallas kernels: 11.5 us -> 7.14 us  [advance(): pl.pallas_call(functools.partial(stage_kernel, sz, stage, last), out_shap...]
where the time goes in v4:
time: 172 us; the launch traced here: 170 us
  waiting for transfers between devices  67.2 us (39%)
  local copies, waits for them, and re-layouts  48.7 us (28%)
  starting transfers between devices  44.8 us (26%)
  Pallas kernels  9.29 us (5%)
    all_to_all x8, waiting for transfers between devices, exchange(): lax.all_to_all(member_out, 'member', split_axis=0, concat_axis=0, tiled=T...  67.2 us
    unnamed x112, local copies, waits for them, and re-layouts  48.7 us
    all_to_all x8, starting transfers between devices, exchange(): lax.all_to_all(member_out, 'member', split_axis=0, concat_axis=0, tiled=T...  32.1 us
    ppermute x8, starting transfers between devices, exchange(): far.append(lax.ppermute(sent, 'group', pairs))  12.7 us
    pallas_call x8, Pallas kernels, advance(): pl.pallas_call(functools.partial(stage_kernel, sz, stage, last), out_shap...  7.14 us
  transfers between devices with their start and end apart: 16, of which 8 were waited for; matrix products, arithmetic and copies ran while one was open for 0% of the time, Pallas kernels for 0%

profile of v4, /device:TPU:0, one launch (start us, length us, event | category | flops | bytes accessed | tf_op | source)
XLA Modules:
  0.0 170.2 jit_solution(16192068000801077537)
XLA Ops:
  0.0 2.1 %begin.1 = (s32[1,128]{1,0:T(1,128)S(4)}, f32[16,64,128]{2,1,0:T(8,128)S(1)}, bf16[16,768,128]{2,1,0:T(8,128)(2,1)S(1)}, f32[16,128]{1,0:T(8,128)S(1)}, bf16[16,...) custom-call(s32[16]{0:T(128)} %refs_0_.1, s32[4,16]{1,0:T(4,128)} %bitcast.4, ...), custom_call_target="tpu_custom_call" | custom-call | tf_op jit(solution)/shard_map/begin/pallas_call | solution.py:168
  4.3 7.4 %all-to-all-start = ((bf16[16,64,128]{2,1,0:T(8,128)(2,1)}), bf16[16,64,128]{2,1,0:T(8,128)(2,1)S(1)}, u32[]{:S(2)}, u32[]{:S(2)}) async-start(bf16[16,64,128]{2,1,0:T(8,128)(2,1)} %copy-done.55), calls=%async_computation | async-start | bytes 524288 | tf_op jit(solution)/shard_map/all_to_all | solution.py:151
  11.7 1.6 collective-permute-start
  13.3 8.4 %all-to-all-done.near = bf16[16,64,128]{2,1,0:T(8,128)(2,1)S(1)} async-done(((bf16[16,64,128]{2,1,0:T(8,128)(2,1)}), bf16[16,64,128]{2,1,0:T(8,128)(2,1)S(1)}, u32[]{:S(2)}, u32[]{:S(2)}) %all-to-all-start) | async-done | bytes 262176 | tf_op jit(solution)/shard_map/all_to_all | solution.py:151
  21.7 1.0 copy-done.5
  22.8 0.9 copy-done.47
  27.6 3.5 %all-to-all-start.1 = ((bf16[16,64,128]{2,1,0:T(8,128)(2,1)}), bf16[16,64,128]{2,1,0:T(8,128)(2,1)S(1)}, u32[]{:S(2)}, u32[]{:S(2)}) async-start(bf16[16,64,128]{2,1,0:T(8,128)(2,1)} %copy-done.53), calls=%async_computation.1 | async-start | bytes 524288 | tf_op jit(solution)/shard_map/all_to_all | solution.py:151
  31.1 1.6 collective-permute-start.1
  32.7 8.4 %all-to-all-done.1.near = bf16[16,64,128]{2,1,0:T(8,128)(2,1)S(1)} async-done(((bf16[16,64,128]{2,1,0:T(8,128)(2,1)}), bf16[16,64,128]{2,1,0:T(8,128)(2,1)S(1)}, u32[]{:S(2)}, u32[]{:S(2)}) %all-to-all-start.1) | async-done | bytes 262176 | tf_op jit(solution)/shard_map/all_to_all | solution.py:151
  41.1 1.0 copy-done.6
  42.1 1.0 copy-done.25
  43.2 1.0 copy-done.27
  44.2 0.9 copy-done.43
  49.0 3.5 %all-to-all-start.2 = ((bf16[16,64,128]{2,1,0:T(8,128)(2,1)}), bf16[16,64,128]{2,1,0:T(8,128)(2,1)S(1)}, u32[]{:S(2)}, u32[]{:S(2)}) async-start(bf16[16,64,128]{2,1,0:T(8,128)(2,1)} %copy-done.50), calls=%async_computation.2 | async-start | bytes 524288 | tf_op jit(solution)/shard_map/all_to_all | solution.py:151
  52.5 1.6 collective-permute-start.2
  54.1 8.4 %all-to-all-done.2.near = bf16[16,64,128]{2,1,0:T(8,128)(2,1)S(1)} async-done(((bf16[16,64,128]{2,1,0:T(8,128)(2,1)}), bf16[16,64,128]{2,1,0:T(8,128)(2,1)S(1)}, u32[]{:S(2)}, u32[]{:S(2)}) %all-to-all-start.2) | async-done | bytes 262176 | tf_op jit(solution)/shard_map/all_to_all | solution.py:151
  62.5 1.0 copy-done.7
  63.6 1.0 copy-done.13
  64.6 1.0 copy-done.15
  65.6 0.9 copy-done.33
  70.4 3.5 %all-to-all-start.3 = ((bf16[16,64,128]{2,1,0:T(8,128)(2,1)}), bf16[16,64,128]{2,1,0:T(8,128)(2,1)S(1)}, u32[]{:S(2)}, u32[]{:S(2)}) async-start(bf16[16,64,128]{2,1,0:T(8,128)(2,1)} %copy-done.48), calls=%async_computation.3 | async-start | bytes 524288 | tf_op jit(solution)/shard_map/all_to_all | solution.py:151
  73.9 1.6 collective-permute-start.3
  75.5 8.4 %all-to-all-done.3.near = bf16[16,64,128]{2,1,0:T(8,128)(2,1)S(1)} async-done(((bf16[16,64,128]{2,1,0:T(8,128)(2,1)}), bf16[16,64,128]{2,1,0:T(8,128)(2,1)S(1)}, u32[]{:S(2)}, u32[]{:S(2)}) %all-to-all-start.3) | async-done | bytes 262176 | tf_op jit(solution)/shard_map/all_to_all | solution.py:151
  83.9 1.0 copy-done.9
  85.0 1.0 copy-done.11
  86.0 0.9 copy-done.37
  89.9 3.5 %all-to-all-start.4 = ((bf16[16,64,128]{2,1,0:T(8,128)(2,1)}), bf16[16,64,128]{2,1,0:T(8,128)(2,1)S(1)}, u32[]{:S(2)}, u32[]{:S(2)}) async-start(bf16[16,64,128]{2,1,0:T(8,128)(2,1)} %copy-done.52), calls=%async_computation.4 | async-start | bytes 524288 | tf_op jit(solution)/shard_map/all_to_all | solution.py:151
  93.5 1.6 collective-permute-start.4
  95.1 8.4 %all-to-all-done.4.near = bf16[16,64,128]{2,1,0:T(8,128)(2,1)S(1)} async-done(((bf16[16,64,128]{2,1,0:T(8,128)(2,1)}), bf16[16,64,128]{2,1,0:T(8,128)(2,1)S(1)}, u32[]{:S(2)}, u32[]{:S(2)}) %all-to-all-start.4) | async-done | bytes 262176 | tf_op jit(solution)/shard_map/all_to_all | solution.py:151
  103.5 1.0 copy-done.1
  109.3 3.5 %all-to-all-start.5 = ((bf16[16,64,128]{2,1,0:T(8,128)(2,1)}), bf16[16,64,128]{2,1,0:T(8,128)(2,1)S(1)}, u32[]{:S(2)}, u32[]{:S(2)}) async-start(bf16[16,64,128]{2,1,0:T(8,128)(2,1)} %copy-done.54), calls=%async_computation.5 | async-start | bytes 524288 | tf_op jit(solution)/shard_map/all_to_all | solution.py:151
  112.8 1.6 collective-permute-start.5
  114.4 8.4 %all-to-all-done.5.near = bf16[16,64,128]{2,1,0:T(8,128)(2,1)S(1)} async-done(((bf16[16,64,128]{2,1,0:T(8,128)(2,1)}), bf16[16,64,128]{2,1,0:T(8,128)(2,1)S(1)}, u32[]{:S(2)}, u32[]{:S(2)}) %all-to-all-start.5) | async-done | bytes 262176 | tf_op jit(solution)/shard_map/all_to_all | solution.py:151
  122.8 1.0 copy-done.2
  123.8 1.0 copy-done.29
  124.9 1.0 copy-done.31
  130.7 3.5 %all-to-all-start.6 = ((bf16[16,64,128]{2,1,0:T(8,128)(2,1)}), bf16[16,64,128]{2,1,0:T(8,128)(2,1)S(1)}, u32[]{:S(2)}, u32[]{:S(2)}) async-start(bf16[16,64,128]{2,1,0:T(8,128)(2,1)} %copy-done.51), calls=%async_computation.6 | async-start | bytes 524288 | tf_op jit(solution)/shard_map/all_to_all | solution.py:151
  134.2 1.6 collective-permute-start.6
  135.8 8.4 %all-to-all-done.6.near = bf16[16,64,128]{2,1,0:T(8,128)(2,1)S(1)} async-done(((bf16[16,64,128]{2,1,0:T(8,128)(2,1)}), bf16[16,64,128]{2,1,0:T(8,128)(2,1)S(1)}, u32[]{:S(2)}, u32[]{:S(2)}) %all-to-all-start.6) | async-done | bytes 262176 | tf_op jit(solution)/shard_map/all_to_all | solution.py:151
  144.2 1.0 copy-done.3
  145.3 1.0 copy-done.17
  146.3 1.0 copy-done.19
  152.1 3.5 %all-to-all-start.7 = ((bf16[16,64,128]{2,1,0:T(8,128)(2,1)}), bf16[16,64,128]{2,1,0:T(8,128)(2,1)S(1)}, u32[]{:S(2)}, u32[]{:S(2)}) async-start(bf16[16,64,128]{2,1,0:T(8,128)(2,1)} %copy-done.49), calls=%async_computation.7 | async-start | bytes 524288 | tf_op jit(solution)/shard_map/all_to_all | solution.py:151
  155.6 1.6 collective-permute-start.7
  157.2 8.4 %all-to-all-done.7.near = bf16[16,64,128]{2,1,0:T(8,128)(2,1)S(1)} async-done(((bf16[16,64,128]{2,1,0:T(8,128)(2,1)}), bf16[16,64,128]{2,1,0:T(8,128)(2,1)S(1)}, u32[]{:S(2)}, u32[]{:S(2)}) %all-to-all-start.7) | async-done | bytes 262176 | tf_op jit(solution)/shard_map/all_to_all | solution.py:151
  165.6 1.0 copy-done.21
  166.7 1.0 copy-done.23
  168.7 1.6 stage.15
  (113 shorter events, 31.8 us)
Async XLA Ops:
  4.3 17.4 %all-to-all-start = ((bf16[16,64,128]{2,1,0:T(8,128)(2,1)}), bf16[16,64,128]{2,1,0:T(8,128)(2,1)S(1)}, u32[]{:S(2)}, u32[]{:S(2)}) async-start(bf16[16,64,128]{2,1,0:T(8,128)(2,1)} %copy-done.55), calls=%async_computation | async-start | bytes 524288 | tf_op jit(solution)/shard_map/all_to_all | solution.py:151
  11.7 10.0 %collective-permute-start = (bf16[2,64,128]{2,1,0:T(8,128)(2,1)S(1)}, bf16[2,64,128]{2,1,0:T(8,128)(2,1)S(1)}, u32[]{:S(2)}, u32[]{:S(2)}) collective-permute-start(bf16[2,64,128]{2,1,0:T(8,128)(2,1)S(1)} %get-tuple-element.51), channel_id=1, source_target_pairs={{0,16},{16,0},{1,17},{17,1},{2,18},{18,2},{3,19},{19,3},{4,20},{20... | collective-permute-start | bytes 98312 | tf_op jit(solution)/shard_map/ppermute | solution.py:150
  21.7 1.0 copy-start.5
  22.8 0.9 copy-start.47
  24.5 0.8 copy-start.24
  25.3 0.8 copy-start.26
  27.6 13.5 %all-to-all-start.1 = ((bf16[16,64,128]{2,1,0:T(8,128)(2,1)}), bf16[16,64,128]{2,1,0:T(8,128)(2,1)S(1)}, u32[]{:S(2)}, u32[]{:S(2)}) async-start(bf16[16,64,128]{2,1,0:T(8,128)(2,1)} %copy-done.53), calls=%async_computation.1 | async-start | bytes 524288 | tf_op jit(solution)/shard_map/all_to_all | solution.py:151
  31.1 10.0 %collective-permute-start.1 = (bf16[2,64,128]{2,1,0:T(8,128)(2,1)S(1)}, bf16[2,64,128]{2,1,0:T(8,128)(2,1)S(1)}, u32[]{:S(2)}, u32[]{:S(2)}) collective-permute-start(bf16[2,64,128]{2,1,0:T(8,128)(2,1)S(1)} %get-tuple-element.55), channel_id=1, source_target_pairs={{0,16},{16,0},{1,17},{17,1},{2,18},{18,2},{3,19},{19,3},{4,20},{20... | collective-permute-start | bytes 98312 | tf_op jit(solution)/shard_map/ppermute | solution.py:150
  41.1 1.0 copy-start.6
  42.1 1.0 copy-start.25
  43.2 1.0 copy-start.27
  44.2 0.9 copy-start.43
  46.0 0.8 copy-start.12
  46.8 0.8 copy-start.14
  49.0 13.5 %all-to-all-start.2 = ((bf16[16,64,128]{2,1,0:T(8,128)(2,1)}), bf16[16,64,128]{2,1,0:T(8,128)(2,1)S(1)}, u32[]{:S(2)}, u32[]{:S(2)}) async-start(bf16[16,64,128]{2,1,0:T(8,128)(2,1)} %copy-done.50), calls=%async_computation.2 | async-start | bytes 524288 | tf_op jit(solution)/shard_map/all_to_all | solution.py:151
  52.5 10.0 %collective-permute-start.2 = (bf16[2,64,128]{2,1,0:T(8,128)(2,1)S(1)}, bf16[2,64,128]{2,1,0:T(8,128)(2,1)S(1)}, u32[]{:S(2)}, u32[]{:S(2)}) collective-permute-start(bf16[2,64,128]{2,1,0:T(8,128)(2,1)S(1)} %get-tuple-element.60), channel_id=1, source_target_pairs={{0,16},{16,0},{1,17},{17,1},{2,18},{18,2},{3,19},{19,3},{4,20},{20... | collective-permute-start | bytes 98312 | tf_op jit(solution)/shard_map/ppermute | solution.py:150
  62.5 1.0 copy-start.7
  63.6 1.0 copy-start.13
  64.6 1.0 copy-start.15
  65.6 0.9 copy-start.33
  70.4 13.5 %all-to-all-start.3 = ((bf16[16,64,128]{2,1,0:T(8,128)(2,1)}), bf16[16,64,128]{2,1,0:T(8,128)(2,1)S(1)}, u32[]{:S(2)}, u32[]{:S(2)}) async-start(bf16[16,64,128]{2,1,0:T(8,128)(2,1)} %copy-done.48), calls=%async_computation.3 | async-start | bytes 524288 | tf_op jit(solution)/shard_map/all_to_all | solution.py:151
  73.9 10.0 %collective-permute-start.3 = (bf16[2,64,128]{2,1,0:T(8,128)(2,1)S(1)}, bf16[2,64,128]{2,1,0:T(8,128)(2,1)S(1)}, u32[]{:S(2)}, u32[]{:S(2)}) collective-permute-start(bf16[2,64,128]{2,1,0:T(8,128)(2,1)S(1)} %get-tuple-element.65), channel_id=1, source_target_pairs={{0,16},{16,0},{1,17},{17,1},{2,18},{18,2},{3,19},{19,3},{4,20},{20... | collective-permute-start | bytes 98312 | tf_op jit(solution)/shard_map/ppermute | solution.py:150
  83.9 1.0 copy-start.9
  85.0 1.0 copy-start.11
  86.0 0.9 copy-start.37
  89.9 13.5 %all-to-all-start.4 = ((bf16[16,64,128]{2,1,0:T(8,128)(2,1)}), bf16[16,64,128]{2,1,0:T(8,128)(2,1)S(1)}, u32[]{:S(2)}, u32[]{:S(2)}) async-start(bf16[16,64,128]{2,1,0:T(8,128)(2,1)} %copy-done.52), calls=%async_computation.4 | async-start | bytes 524288 | tf_op jit(solution)/shard_map/all_to_all | solution.py:151
  93.5 10.0 %collective-permute-start.4 = (bf16[2,64,128]{2,1,0:T(8,128)(2,1)S(1)}, bf16[2,64,128]{2,1,0:T(8,128)(2,1)S(1)}, u32[]{:S(2)}, u32[]{:S(2)}) collective-permute-start(bf16[2,64,128]{2,1,0:T(8,128)(2,1)S(1)} %get-tuple-element.70), channel_id=1, source_target_pairs={{0,16},{16,0},{1,17},{17,1},{2,18},{18,2},{3,19},{19,3},{4,20},{20... | collective-permute-start | bytes 98312 | tf_op jit(solution)/shard_map/ppermute | solution.py:150
  103.4 1.0 copy-start.1
  104.5 0.9 copy-start.39
  107.0 0.8 copy-start.30
  109.3 13.5 %all-to-all-start.5 = ((bf16[16,64,128]{2,1,0:T(8,128)(2,1)}), bf16[16,64,128]{2,1,0:T(8,128)(2,1)S(1)}, u32[]{:S(2)}, u32[]{:S(2)}) async-start(bf16[16,64,128]{2,1,0:T(8,128)(2,1)} %copy-done.54), calls=%async_computation.5 | async-start | bytes 524288 | tf_op jit(solution)/shard_map/all_to_all | solution.py:151
  112.8 10.0 %collective-permute-start.5 = (bf16[2,64,128]{2,1,0:T(8,128)(2,1)S(1)}, bf16[2,64,128]{2,1,0:T(8,128)(2,1)S(1)}, u32[]{:S(2)}, u32[]{:S(2)}) collective-permute-start(bf16[2,64,128]{2,1,0:T(8,128)(2,1)S(1)} %get-tuple-element.74), channel_id=1, source_target_pairs={{0,16},{16,0},{1,17},{17,1},{2,18},{18,2},{3,19},{19,3},{4,20},{20... | collective-permute-start | bytes 98312 | tf_op jit(solution)/shard_map/ppermute | solution.py:150
  122.8 1.0 copy-start.2
  123.8 1.0 copy-start.29
  124.9 1.0 copy-start.31
  125.9 0.9 copy-start.45
  128.5 0.8 copy-start.18
  130.7 13.5 %all-to-all-start.6 = ((bf16[16,64,128]{2,1,0:T(8,128)(2,1)}), bf16[16,64,128]{2,1,0:T(8,128)(2,1)S(1)}, u32[]{:S(2)}, u32[]{:S(2)}) async-start(bf16[16,64,128]{2,1,0:T(8,128)(2,1)} %copy-done.51), calls=%async_computation.6 | async-start | bytes 524288 | tf_op jit(solution)/shard_map/all_to_all | solution.py:151
  134.2 10.0 %collective-permute-start.6 = (bf16[2,64,128]{2,1,0:T(8,128)(2,1)S(1)}, bf16[2,64,128]{2,1,0:T(8,128)(2,1)S(1)}, u32[]{:S(2)}, u32[]{:S(2)}) collective-permute-start(bf16[2,64,128]{2,1,0:T(8,128)(2,1)S(1)} %get-tuple-element.79), channel_id=1, source_target_pairs={{0,16},{16,0},{1,17},{17,1},{2,18},{18,2},{3,19},{19,3},{4,20},{20... | collective-permute-start | bytes 98312 | tf_op jit(solution)/shard_map/ppermute | solution.py:150
  144.2 1.0 copy-start.3
  145.3 1.0 copy-start.17
  146.3 1.0 copy-start.19
  147.3 0.9 copy-start.35
  152.1 13.5 %all-to-all-start.7 = ((bf16[16,64,128]{2,1,0:T(8,128)(2,1)}), bf16[16,64,128]{2,1,0:T(8,128)(2,1)S(1)}, u32[]{:S(2)}, u32[]{:S(2)}) async-start(bf16[16,64,128]{2,1,0:T(8,128)(2,1)} %copy-done.49), calls=%async_computation.7 | async-start | bytes 524288 | tf_op jit(solution)/shard_map/all_to_all | solution.py:151
  155.6 10.0 %collective-permute-start.7 = (bf16[2,64,128]{2,1,0:T(8,128)(2,1)S(1)}, bf16[2,64,128]{2,1,0:T(8,128)(2,1)S(1)}, u32[]{:S(2)}, u32[]{:S(2)}) collective-permute-start(bf16[2,64,128]{2,1,0:T(8,128)(2,1)S(1)} %get-tuple-element.84), channel_id=1, source_target_pairs={{0,16},{16,0},{1,17},{17,1},{2,18},{18,2},{3,19},{19,3},{4,20},{20... | collective-permute-start | bytes 98312 | tf_op jit(solution)/shard_map/ppermute | solution.py:150
  165.6 1.0 copy-start.21
  166.7 1.0 copy-start.23
  167.7 0.9 copy-start.41
  (24 other events, 17.6 us)

commit v5 on v4

--- a/solution.py
+++ b/solution.py
@@ -49,14 +49,14 @@
 
 
 def first_kernel(sz, *refs):
-    indices_far, (state_far, blocks_far, rate_far), refs = refs[:5], refs[5:8], refs[8:]
-    (table, state, blocks, rate, rounded, member_out, group_out), refs = refs[:7], refs[7:]
+    indices_far, (state_far, rate_far), refs = refs[:5], refs[5:7], refs[7:]
+    (table, state, rate, rounded, member_out, group_out), refs = refs[:6], refs[6:]
     indices, sems = refs[:5], refs[5]
     own_col, near_col, far_col, member_send, group_send = indices
     copies = [
         pltpu.make_async_copy(source, target, sems.at[n])
         for n, (source, target) in enumerate(
-            zip((state_far, rate_far, *indices_far, blocks_far), (state, rate, *indices, blocks))
+            zip((state_far, rate_far, *indices_far), (state, rate, *indices))
         )
     ]
     for copy in copies:
@@ -81,7 +81,6 @@
         rounded[i] = state[i].astype(jnp.bfloat16)
     fill_sends(sz, table, rounded, member_out, group_out)
     copies[1].wait()
-    copies[7].wait()
 
 
 def stage_kernel(sz, stage, last, *refs):
@@ -134,7 +133,7 @@
         sz = Sizes(mesh, state, member_col, group_col, group_send)
         far_off = lambda x: pltpu.with_memory_space_constraint(x, pltpu.MemorySpace.HBM)
         held = lambda x: pltpu.VMEM(x.shape, x.dtype)
-        weights = far_off(blocks.reshape(sz.rows, -1, sz.cells))
+        weights = blocks.reshape(sz.rows, -1, sz.cells)
         entries = -(-(sz.at_group + 1) // 128) * 128
         f32 = jax.ShapeDtypeStruct((sz.rows, sz.traj, sz.cells), jnp.float32)
         bf16 = lambda n: jax.ShapeDtypeStruct((n, sz.traj, sz.cells), jnp.bfloat16)
@@ -167,17 +166,18 @@
             tables = [own_col, member_col.T, group_col.T, member_send, group_send]
             return pl.pallas_call(
                 functools.partial(first_kernel, sz),
-                out_shape=[pltpu.SMEM((1, entries), jnp.int32), held(state), held(weights), held(rate), *sends],
-                in_specs=[ANY] * 8,
-                out_specs=[SMEM] + [VMEM] * 6,
-                scratch_shapes=[pltpu.SMEM(x.shape, x.dtype) for x in tables] + [pltpu.SemaphoreType.DMA((8,))],
+                out_shape=[pltpu.SMEM((1, entries), jnp.int32), held(state), held(rate), *sends],
+                in_specs=[ANY] * 7,
+                out_specs=[SMEM] + [VMEM] * 5,
+                scratch_shapes=[pltpu.SMEM(x.shape, x.dtype) for x in tables] + [pltpu.SemaphoreType.DMA((7,))],
                 compiler_params=pltpu.CompilerParams(vmem_limit_bytes=limit),
+                cost_estimate=pl.CostEstimate(flops=4 * flops, bytes_accessed=state.size * 4, transcendentals=0),
                 name="begin",
-            )(*map(far_off, tables), far_off(state), weights, far_off(rate))
+            )(*map(far_off, tables), far_off(state), far_off(rate))
 
         def advance(stage, last, carry, near, far):
             rounded, base, value, total = carry
-            ops = [table, held_weights, held_rate, rounded, near, far]
+            ops = [table, weights, held_rate, rounded, near, far]
             if stage < 3:
                 ops.append(base)
             if stage > 0:
@@ -199,7 +199,7 @@
                 return (got[0], base, got[3], got[4]), got[1], got[2]
             return (got[0], got[3], None, None), got[1], got[2]
 
-        table, base, held_weights, held_rate, rounded, member_out, group_out = begin()
+        table, base, held_rate, rounded, member_out, group_out = begin()
         carry = (rounded, base, None, None)
         for step in range(STEPS):
             for stage in range(4):

time: 172 us -> 171 us (level)
    unnamed x112 -> x114, local copies, waits for them, and re-layouts: 48.7 us -> 48.6 us
where the time goes in v5:
time: 171 us; the launch traced here: 169 us
  waiting for transfers between devices  67.2 us (39%)
  local copies, waits for them, and re-layouts  48.6 us (28%)
  starting transfers between devices  44.8 us (26%)
  Pallas kernels  8.45 us (5%)
    all_to_all x8, waiting for transfers between devices, exchange(): lax.all_to_all(member_out, 'member', split_axis=0, concat_axis=0, tiled=T...  67.2 us
    unnamed x114, local copies, waits for them, and re-layouts  48.6 us
    all_to_all x8, starting transfers between devices, exchange(): lax.all_to_all(member_out, 'member', split_axis=0, concat_axis=0, tiled=T...  32.1 us
    ppermute x8, starting transfers between devices, exchange(): far.append(lax.ppermute(sent, 'group', pairs))  12.7 us
    pallas_call x8, Pallas kernels, advance(): pl.pallas_call(functools.partial(stage_kernel, sz, stage, last), out_shap...  7.15 us
  transfers between devices with their start and end apart: 16, of which 8 were waited for; matrix products, arithmetic and copies ran while one was open for 0% of the time, Pallas kernels for 0%

profile of v5, /device:TPU:0, one launch (start us, length us, event | category | flops | bytes accessed | tf_op | source)
XLA Modules:
  0.0 169.3 jit_solution(16343995615662189102)
XLA Ops:
  0.0 1.3 begin.1
  3.5 7.4 %all-to-all-start = ((bf16[16,64,128]{2,1,0:T(8,128)(2,1)}), bf16[16,64,128]{2,1,0:T(8,128)(2,1)S(1)}, u32[]{:S(2)}, u32[]{:S(2)}) async-start(bf16[16,64,128]{2,1,0:T(8,128)(2,1)} %copy-done.56), calls=%async_computation | async-start | bytes 524288 | tf_op jit(solution)/shard_map/all_to_all | solution.py:150
  10.9 1.6 collective-permute-start
  12.5 8.4 %all-to-all-done.near = bf16[16,64,128]{2,1,0:T(8,128)(2,1)S(1)} async-done(((bf16[16,64,128]{2,1,0:T(8,128)(2,1)}), bf16[16,64,128]{2,1,0:T(8,128)(2,1)S(1)}, u32[]{:S(2)}, u32[]{:S(2)}) %all-to-all-start) | async-done | bytes 262176 | tf_op jit(solution)/shard_map/all_to_all | solution.py:150
  20.9 1.0 copy-done.6
  22.0 0.9 copy-done.48
  26.7 3.5 %all-to-all-start.1 = ((bf16[16,64,128]{2,1,0:T(8,128)(2,1)}), bf16[16,64,128]{2,1,0:T(8,128)(2,1)S(1)}, u32[]{:S(2)}, u32[]{:S(2)}) async-start(bf16[16,64,128]{2,1,0:T(8,128)(2,1)} %copy-done.54), calls=%async_computation.1 | async-start | bytes 524288 | tf_op jit(solution)/shard_map/all_to_all | solution.py:150
  30.3 1.6 collective-permute-start.1
  31.8 8.4 %all-to-all-done.1.near = bf16[16,64,128]{2,1,0:T(8,128)(2,1)S(1)} async-done(((bf16[16,64,128]{2,1,0:T(8,128)(2,1)}), bf16[16,64,128]{2,1,0:T(8,128)(2,1)S(1)}, u32[]{:S(2)}, u32[]{:S(2)}) %all-to-all-start.1) | async-done | bytes 262176 | tf_op jit(solution)/shard_map/all_to_all | solution.py:150
  40.2 1.0 copy-done.7
  41.3 1.0 copy-done.22
  42.3 1.0 copy-done.24
  43.4 0.9 copy-done.42
  48.1 3.5 %all-to-all-start.2 = ((bf16[16,64,128]{2,1,0:T(8,128)(2,1)}), bf16[16,64,128]{2,1,0:T(8,128)(2,1)S(1)}, u32[]{:S(2)}, u32[]{:S(2)}) async-start(bf16[16,64,128]{2,1,0:T(8,128)(2,1)} %copy-done.51), calls=%async_computation.2 | async-start | bytes 524288 | tf_op jit(solution)/shard_map/all_to_all | solution.py:150
  51.7 1.6 collective-permute-start.2
  53.2 8.4 %all-to-all-done.2.near = bf16[16,64,128]{2,1,0:T(8,128)(2,1)S(1)} async-done(((bf16[16,64,128]{2,1,0:T(8,128)(2,1)}), bf16[16,64,128]{2,1,0:T(8,128)(2,1)S(1)}, u32[]{:S(2)}, u32[]{:S(2)}) %all-to-all-start.2) | async-done | bytes 262176 | tf_op jit(solution)/shard_map/all_to_all | solution.py:150
  61.6 1.0 copy-done.8
  62.7 1.0 copy-done.14
  63.7 1.0 copy-done.16
  69.5 3.5 %all-to-all-start.3 = ((bf16[16,64,128]{2,1,0:T(8,128)(2,1)}), bf16[16,64,128]{2,1,0:T(8,128)(2,1)S(1)}, u32[]{:S(2)}, u32[]{:S(2)}) async-start(bf16[16,64,128]{2,1,0:T(8,128)(2,1)} %copy-done.49), calls=%async_computation.3 | async-start | bytes 524288 | tf_op jit(solution)/shard_map/all_to_all | solution.py:150
  73.1 1.6 collective-permute-start.3
  74.7 8.4 %all-to-all-done.3.near = bf16[16,64,128]{2,1,0:T(8,128)(2,1)S(1)} async-done(((bf16[16,64,128]{2,1,0:T(8,128)(2,1)}), bf16[16,64,128]{2,1,0:T(8,128)(2,1)S(1)}, u32[]{:S(2)}, u32[]{:S(2)}) %all-to-all-start.3) | async-done | bytes 262176 | tf_op jit(solution)/shard_map/all_to_all | solution.py:150
  83.1 1.0 copy-done.10
  84.1 1.0 copy-done.12
  85.1 0.9 copy-done.38
  89.1 3.5 %all-to-all-start.4 = ((bf16[16,64,128]{2,1,0:T(8,128)(2,1)}), bf16[16,64,128]{2,1,0:T(8,128)(2,1)S(1)}, u32[]{:S(2)}, u32[]{:S(2)}) async-start(bf16[16,64,128]{2,1,0:T(8,128)(2,1)} %copy-done.53), calls=%async_computation.4 | async-start | bytes 524288 | tf_op jit(solution)/shard_map/all_to_all | solution.py:150
  92.6 1.6 collective-permute-start.4
  94.2 8.4 %all-to-all-done.4.near = bf16[16,64,128]{2,1,0:T(8,128)(2,1)S(1)} async-done(((bf16[16,64,128]{2,1,0:T(8,128)(2,1)}), bf16[16,64,128]{2,1,0:T(8,128)(2,1)S(1)}, u32[]{:S(2)}, u32[]{:S(2)}) %all-to-all-start.4) | async-done | bytes 262176 | tf_op jit(solution)/shard_map/all_to_all | solution.py:150
  102.6 1.0 copy-done.2
  103.7 0.9 copy-done.40
  108.4 3.5 %all-to-all-start.5 = ((bf16[16,64,128]{2,1,0:T(8,128)(2,1)}), bf16[16,64,128]{2,1,0:T(8,128)(2,1)S(1)}, u32[]{:S(2)}, u32[]{:S(2)}) async-start(bf16[16,64,128]{2,1,0:T(8,128)(2,1)} %copy-done.55), calls=%async_computation.5 | async-start | bytes 524288 | tf_op jit(solution)/shard_map/all_to_all | solution.py:150
  111.9 1.6 collective-permute-start.5
  113.5 8.4 %all-to-all-done.5.near = bf16[16,64,128]{2,1,0:T(8,128)(2,1)S(1)} async-done(((bf16[16,64,128]{2,1,0:T(8,128)(2,1)}), bf16[16,64,128]{2,1,0:T(8,128)(2,1)S(1)}, u32[]{:S(2)}, u32[]{:S(2)}) %all-to-all-start.5) | async-done | bytes 262176 | tf_op jit(solution)/shard_map/all_to_all | solution.py:150
  121.9 1.0 copy-done.3
  123.0 1.0 copy-done.26
  124.0 1.0 copy-done.28
  129.8 3.5 %all-to-all-start.6 = ((bf16[16,64,128]{2,1,0:T(8,128)(2,1)}), bf16[16,64,128]{2,1,0:T(8,128)(2,1)S(1)}, u32[]{:S(2)}, u32[]{:S(2)}) async-start(bf16[16,64,128]{2,1,0:T(8,128)(2,1)} %copy-done.52), calls=%async_computation.6 | async-start | bytes 524288 | tf_op jit(solution)/shard_map/all_to_all | solution.py:150
  133.3 1.6 collective-permute-start.6
  134.9 8.4 %all-to-all-done.6.near = bf16[16,64,128]{2,1,0:T(8,128)(2,1)S(1)} async-done(((bf16[16,64,128]{2,1,0:T(8,128)(2,1)}), bf16[16,64,128]{2,1,0:T(8,128)(2,1)S(1)}, u32[]{:S(2)}, u32[]{:S(2)}) %all-to-all-start.6) | async-done | bytes 262176 | tf_op jit(solution)/shard_map/all_to_all | solution.py:150
  143.3 1.0 copy-done.4
  144.4 1.0 copy-done.18
  145.4 1.0 copy-done.20
  151.2 3.5 %all-to-all-start.7 = ((bf16[16,64,128]{2,1,0:T(8,128)(2,1)}), bf16[16,64,128]{2,1,0:T(8,128)(2,1)S(1)}, u32[]{:S(2)}, u32[]{:S(2)}) async-start(bf16[16,64,128]{2,1,0:T(8,128)(2,1)} %copy-done.50), calls=%async_computation.7 | async-start | bytes 524288 | tf_op jit(solution)/shard_map/all_to_all | solution.py:150
  154.8 1.6 collective-permute-start.7
  156.3 8.4 %all-to-all-done.7.near = bf16[16,64,128]{2,1,0:T(8,128)(2,1)S(1)} async-done(((bf16[16,64,128]{2,1,0:T(8,128)(2,1)}), bf16[16,64,128]{2,1,0:T(8,128)(2,1)S(1)}, u32[]{:S(2)}, u32[]{:S(2)}) %all-to-all-start.7) | async-done | bytes 262176 | tf_op jit(solution)/shard_map/all_to_all | solution.py:150
  164.7 1.0 copy-done.30
  165.8 1.0 copy-done.32
  167.8 1.6 stage.15
  (115 shorter events, 31.7 us)
Async XLA Ops:
  0.0 20.9 %copy-start = (bf16[16,6,128,128]{3,2,1,0:T(8,128)(2,1)S(1)}, bf16[16,6,128,128]{3,2,1,0:T(8,128)(2,1)}, u32[]{:S(2)}) copy-start(bf16[16,6,128,128]{3,2,1,0:T(8,128)(2,1)} %param.9) | copy-start | bytes 9437188
  1.3 0.8 copy-start.5
  3.5 17.4 %all-to-all-start = ((bf16[16,64,128]{2,1,0:T(8,128)(2,1)}), bf16[16,64,128]{2,1,0:T(8,128)(2,1)S(1)}, u32[]{:S(2)}, u32[]{:S(2)}) async-start(bf16[16,64,128]{2,1,0:T(8,128)(2,1)} %copy-done.56), calls=%async_computation | async-start | bytes 524288 | tf_op jit(solution)/shard_map/all_to_all | solution.py:150
  10.9 10.0 %collective-permute-start = (bf16[2,64,128]{2,1,0:T(8,128)(2,1)S(1)}, bf16[2,64,128]{2,1,0:T(8,128)(2,1)S(1)}, u32[]{:S(2)}, u32[]{:S(2)}) collective-permute-start(bf16[2,64,128]{2,1,0:T(8,128)(2,1)S(1)} %get-tuple-element.49), channel_id=1, source_target_pairs={{0,16},{16,0},{1,17},{17,1},{2,18},{18,2},{3,19},{19,3},{4,20},{20... | collective-permute-start | bytes 98312 | tf_op jit(solution)/shard_map/ppermute | solution.py:149
  20.9 1.0 copy-start.6
  22.0 0.9 copy-start.48
  24.5 0.8 copy-start.23
  26.7 13.5 %all-to-all-start.1 = ((bf16[16,64,128]{2,1,0:T(8,128)(2,1)}), bf16[16,64,128]{2,1,0:T(8,128)(2,1)S(1)}, u32[]{:S(2)}, u32[]{:S(2)}) async-start(bf16[16,64,128]{2,1,0:T(8,128)(2,1)} %copy-done.54), calls=%async_computation.1 | async-start | bytes 524288 | tf_op jit(solution)/shard_map/all_to_all | solution.py:150
  30.3 10.0 %collective-permute-start.1 = (bf16[2,64,128]{2,1,0:T(8,128)(2,1)S(1)}, bf16[2,64,128]{2,1,0:T(8,128)(2,1)S(1)}, u32[]{:S(2)}, u32[]{:S(2)}) collective-permute-start(bf16[2,64,128]{2,1,0:T(8,128)(2,1)S(1)} %get-tuple-element.53), channel_id=1, source_target_pairs={{0,16},{16,0},{1,17},{17,1},{2,18},{18,2},{3,19},{19,3},{4,20},{20... | collective-permute-start | bytes 98312 | tf_op jit(solution)/shard_map/ppermute | solution.py:149
  40.2 1.0 copy-start.7
  41.3 1.0 copy-start.22
  42.3 1.0 copy-start.24
  43.4 0.9 copy-start.42
  45.9 0.8 copy-start.15
  48.1 13.5 %all-to-all-start.2 = ((bf16[16,64,128]{2,1,0:T(8,128)(2,1)}), bf16[16,64,128]{2,1,0:T(8,128)(2,1)S(1)}, u32[]{:S(2)}, u32[]{:S(2)}) async-start(bf16[16,64,128]{2,1,0:T(8,128)(2,1)} %copy-done.51), calls=%async_computation.2 | async-start | bytes 524288 | tf_op jit(solution)/shard_map/all_to_all | solution.py:150
  51.7 10.0 %collective-permute-start.2 = (bf16[2,64,128]{2,1,0:T(8,128)(2,1)S(1)}, bf16[2,64,128]{2,1,0:T(8,128)(2,1)S(1)}, u32[]{:S(2)}, u32[]{:S(2)}) collective-permute-start(bf16[2,64,128]{2,1,0:T(8,128)(2,1)S(1)} %get-tuple-element.58), channel_id=1, source_target_pairs={{0,16},{16,0},{1,17},{17,1},{2,18},{18,2},{3,19},{19,3},{4,20},{20... | collective-permute-start | bytes 98312 | tf_op jit(solution)/shard_map/ppermute | solution.py:149
  61.6 1.0 copy-start.8
  62.7 1.0 copy-start.14
  63.7 1.0 copy-start.16
  64.8 0.9 copy-start.34
  69.5 13.5 %all-to-all-start.3 = ((bf16[16,64,128]{2,1,0:T(8,128)(2,1)}), bf16[16,64,128]{2,1,0:T(8,128)(2,1)S(1)}, u32[]{:S(2)}, u32[]{:S(2)}) async-start(bf16[16,64,128]{2,1,0:T(8,128)(2,1)} %copy-done.49), calls=%async_computation.3 | async-start | bytes 524288 | tf_op jit(solution)/shard_map/all_to_all | solution.py:150
  73.1 10.0 %collective-permute-start.3 = (bf16[2,64,128]{2,1,0:T(8,128)(2,1)S(1)}, bf16[2,64,128]{2,1,0:T(8,128)(2,1)S(1)}, u32[]{:S(2)}, u32[]{:S(2)}) collective-permute-start(bf16[2,64,128]{2,1,0:T(8,128)(2,1)S(1)} %get-tuple-element.63), channel_id=1, source_target_pairs={{0,16},{16,0},{1,17},{17,1},{2,18},{18,2},{3,19},{19,3},{4,20},{20... | collective-permute-start | bytes 98312 | tf_op jit(solution)/shard_map/ppermute | solution.py:149
  83.1 1.0 copy-start.10
  84.1 1.0 copy-start.12
  85.1 0.9 copy-start.38
  89.1 13.5 %all-to-all-start.4 = ((bf16[16,64,128]{2,1,0:T(8,128)(2,1)}), bf16[16,64,128]{2,1,0:T(8,128)(2,1)S(1)}, u32[]{:S(2)}, u32[]{:S(2)}) async-start(bf16[16,64,128]{2,1,0:T(8,128)(2,1)} %copy-done.53), calls=%async_computation.4 | async-start | bytes 524288 | tf_op jit(solution)/shard_map/all_to_all | solution.py:150
  92.6 10.0 %collective-permute-start.4 = (bf16[2,64,128]{2,1,0:T(8,128)(2,1)S(1)}, bf16[2,64,128]{2,1,0:T(8,128)(2,1)S(1)}, u32[]{:S(2)}, u32[]{:S(2)}) collective-permute-start(bf16[2,64,128]{2,1,0:T(8,128)(2,1)S(1)} %get-tuple-element.68), channel_id=1, source_target_pairs={{0,16},{16,0},{1,17},{17,1},{2,18},{18,2},{3,19},{19,3},{4,20},{20... | collective-permute-start | bytes 98312 | tf_op jit(solution)/shard_map/ppermute | solution.py:149
  102.6 1.0 copy-start.2
  103.6 0.9 copy-start.40
  106.2 0.8 copy-start.27
  108.4 13.5 %all-to-all-start.5 = ((bf16[16,64,128]{2,1,0:T(8,128)(2,1)}), bf16[16,64,128]{2,1,0:T(8,128)(2,1)S(1)}, u32[]{:S(2)}, u32[]{:S(2)}) async-start(bf16[16,64,128]{2,1,0:T(8,128)(2,1)} %copy-done.55), calls=%async_computation.5 | async-start | bytes 524288 | tf_op jit(solution)/shard_map/all_to_all | solution.py:150
  111.9 10.0 %collective-permute-start.5 = (bf16[2,64,128]{2,1,0:T(8,128)(2,1)S(1)}, bf16[2,64,128]{2,1,0:T(8,128)(2,1)S(1)}, u32[]{:S(2)}, u32[]{:S(2)}) collective-permute-start(bf16[2,64,128]{2,1,0:T(8,128)(2,1)S(1)} %get-tuple-element.72), channel_id=1, source_target_pairs={{0,16},{16,0},{1,17},{17,1},{2,18},{18,2},{3,19},{19,3},{4,20},{20... | collective-permute-start | bytes 98312 | tf_op jit(solution)/shard_map/ppermute | solution.py:149
  121.9 1.0 copy-start.3
  123.0 1.0 copy-start.26
  124.0 1.0 copy-start.28
  125.1 0.9 copy-start.44
  127.6 0.8 copy-start.19
  129.8 13.5 %all-to-all-start.6 = ((bf16[16,64,128]{2,1,0:T(8,128)(2,1)}), bf16[16,64,128]{2,1,0:T(8,128)(2,1)S(1)}, u32[]{:S(2)}, u32[]{:S(2)}) async-start(bf16[16,64,128]{2,1,0:T(8,128)(2,1)} %copy-done.52), calls=%async_computation.6 | async-start | bytes 524288 | tf_op jit(solution)/shard_map/all_to_all | solution.py:150
  133.3 10.0 %collective-permute-start.6 = (bf16[2,64,128]{2,1,0:T(8,128)(2,1)S(1)}, bf16[2,64,128]{2,1,0:T(8,128)(2,1)S(1)}, u32[]{:S(2)}, u32[]{:S(2)}) collective-permute-start(bf16[2,64,128]{2,1,0:T(8,128)(2,1)S(1)} %get-tuple-element.77), channel_id=1, source_target_pairs={{0,16},{16,0},{1,17},{17,1},{2,18},{18,2},{3,19},{19,3},{4,20},{20... | collective-permute-start | bytes 98312 | tf_op jit(solution)/shard_map/ppermute | solution.py:149
  143.3 1.0 copy-start.4
  144.4 1.0 copy-start.18
  145.4 1.0 copy-start.20
  146.5 0.9 copy-start.36
  151.2 13.5 %all-to-all-start.7 = ((bf16[16,64,128]{2,1,0:T(8,128)(2,1)}), bf16[16,64,128]{2,1,0:T(8,128)(2,1)S(1)}, u32[]{:S(2)}, u32[]{:S(2)}) async-start(bf16[16,64,128]{2,1,0:T(8,128)(2,1)} %copy-done.50), calls=%async_computation.7 | async-start | bytes 524288 | tf_op jit(solution)/shard_map/all_to_all | solution.py:150
  154.8 10.0 %collective-permute-start.7 = (bf16[2,64,128]{2,1,0:T(8,128)(2,1)S(1)}, bf16[2,64,128]{2,1,0:T(8,128)(2,1)S(1)}, u32[]{:S(2)}, u32[]{:S(2)}) collective-permute-start(bf16[2,64,128]{2,1,0:T(8,128)(2,1)S(1)} %get-tuple-element.82), channel_id=1, source_target_pairs={{0,16},{16,0},{1,17},{17,1},{2,18},{18,2},{3,19},{19,3},{4,20},{20... | collective-permute-start | bytes 98312 | tf_op jit(solution)/shard_map/ppermute | solution.py:149
  164.7 1.0 copy-start.30
  165.8 1.0 copy-start.32
  166.8 0.9 copy-start.46
  (25 other events, 18.4 us)

commit v6 on v5

--- a/solution.py
+++ b/solution.py
@@ -24,6 +24,7 @@
         self.groups = mesh.shape["group"]
         self.members = mesh.shape["member"]
         self.rows, self.traj, self.cells = state.shape
+        self.burst = 4 if self.rows % 4 == 0 else 1
         self.near = member_col.shape[1]
         self.far = group_col.shape[1]
         self.sent = group_send.shape[1] // self.groups
@@ -94,6 +95,9 @@
     out = next(it)
     total_out = next(it) if stage < 3 else None
     far_all = next(it)
+    if last:
+        whole, out, sems = out, *it
+    finals = []
 
     for slot in range(sz.sent):
         far_all[slot] = rounded[group_row(sz, table, 0, slot)]
@@ -122,10 +126,16 @@
         else:
             fresh = total[i] + (step_size / 6.0) * slope
         out[i] = fresh
+        if last and (i + 1) % sz.burst == 0:
+            done = pl.ds(i + 1 - sz.burst, sz.burst)
+            finals.append(pltpu.make_async_copy(out.at[done], whole.at[done], sems.at[i // sz.burst]))
+            finals[-1].start()
         if not last:
             rounded_out[i] = fresh.astype(jnp.bfloat16)
     if not last:
         fill_sends(sz, table, rounded_out, member_out, group_out)
+    for copy in finals:
+        copy.wait()
 
 
 def solution(mesh):
@@ -182,13 +192,15 @@
                 ops.append(base)
             if stage > 0:
                 ops += [value, total]
-            outs = ([] if last else list(sends)) + [f32] + ([f32] if stage < 3 else [])
+            outs = [state] if last else [*sends, f32] + ([f32] if stage < 3 else [])
+            outs = [jax.ShapeDtypeStruct(x.shape, x.dtype) if last else x for x in outs]
+            extra = [pltpu.VMEM(state.shape, state.dtype), pltpu.SemaphoreType.DMA((sz.rows // sz.burst,))] if last else []
             got = pl.pallas_call(
                 functools.partial(stage_kernel, sz, stage, last),
                 out_shape=outs,
                 in_specs=[SMEM] + [VMEM] * (len(ops) - 1),
-                out_specs=[VMEM] * len(outs),
-                scratch_shapes=[pltpu.VMEM((sz.groups * sz.sent, sz.traj, sz.cells), jnp.bfloat16)],
+                out_specs=[ANY if last else VMEM] * len(outs),
+                scratch_shapes=[pltpu.VMEM((sz.groups * sz.sent, sz.traj, sz.cells), jnp.bfloat16), *extra],
                 compiler_params=pltpu.CompilerParams(vmem_limit_bytes=limit),
                 cost_estimate=pl.CostEstimate(flops=flops, bytes_accessed=weights.size * 2, transcendentals=0),
                 name="stage",

time: 171 us -> 171 us (level)
  no operation moved by 1% of the time
where the time goes in v6:
time: 171 us; the launch traced here: 169 us
  waiting for transfers between devices  67.2 us (39%)
  local copies, waits for them, and re-layouts  48.6 us (28%)
  starting transfers between devices  44.8 us (26%)
  Pallas kernels  8.35 us (5%)
    all_to_all x8, waiting for transfers between devices, exchange(): lax.all_to_all(member_out, 'member', split_axis=0, concat_axis=0, tiled=T...  67.2 us
    unnamed x114, local copies, waits for them, and re-layouts  48.6 us
    all_to_all x8, starting transfers between devices, exchange(): lax.all_to_all(member_out, 'member', split_axis=0, concat_axis=0, tiled=T...  32.1 us
    ppermute x8, starting transfers between devices, exchange(): far.append(lax.ppermute(sent, 'group', pairs))  12.7 us
    pallas_call x8, Pallas kernels, advance(): pl.pallas_call(functools.partial(stage_kernel, sz, stage, last), out_shap...  7.04 us
  transfers between devices with their start and end apart: 16, of which 8 were waited for; matrix products, arithmetic and copies ran while one was open for 0% of the time, Pallas kernels for 0%

profile of v6, /device:TPU:0, one launch (start us, length us, event | category | flops | bytes accessed | tf_op | source)
XLA Modules:
  0.0 169.2 jit_solution(7844992991214415640)
XLA Ops:
  0.0 1.3 begin.1
  3.5 7.4 %all-to-all-start = ((bf16[16,64,128]{2,1,0:T(8,128)(2,1)}), bf16[16,64,128]{2,1,0:T(8,128)(2,1)S(1)}, u32[]{:S(2)}, u32[]{:S(2)}) async-start(bf16[16,64,128]{2,1,0:T(8,128)(2,1)} %copy-done.56), calls=%async_computation | async-start | bytes 524288 | tf_op jit(solution)/shard_map/all_to_all | solution.py:160
  10.9 1.6 collective-permute-start
  12.5 8.4 %all-to-all-done.near = bf16[16,64,128]{2,1,0:T(8,128)(2,1)S(1)} async-done(((bf16[16,64,128]{2,1,0:T(8,128)(2,1)}), bf16[16,64,128]{2,1,0:T(8,128)(2,1)S(1)}, u32[]{:S(2)}, u32[]{:S(2)}) %all-to-all-start) | async-done | bytes 262176 | tf_op jit(solution)/shard_map/all_to_all | solution.py:160
  20.9 1.0 copy-done.6
  22.0 0.9 copy-done.48
  26.7 3.5 %all-to-all-start.1 = ((bf16[16,64,128]{2,1,0:T(8,128)(2,1)}), bf16[16,64,128]{2,1,0:T(8,128)(2,1)S(1)}, u32[]{:S(2)}, u32[]{:S(2)}) async-start(bf16[16,64,128]{2,1,0:T(8,128)(2,1)} %copy-done.54), calls=%async_computation.1 | async-start | bytes 524288 | tf_op jit(solution)/shard_map/all_to_all | solution.py:160
  30.3 1.6 collective-permute-start.1
  31.8 8.4 %all-to-all-done.1.near = bf16[16,64,128]{2,1,0:T(8,128)(2,1)S(1)} async-done(((bf16[16,64,128]{2,1,0:T(8,128)(2,1)}), bf16[16,64,128]{2,1,0:T(8,128)(2,1)S(1)}, u32[]{:S(2)}, u32[]{:S(2)}) %all-to-all-start.1) | async-done | bytes 262176 | tf_op jit(solution)/shard_map/all_to_all | solution.py:160
  40.2 1.0 copy-done.7
  41.3 1.0 copy-done.22
  42.3 1.0 copy-done.24
  43.4 0.9 copy-done.42
  48.1 3.5 %all-to-all-start.2 = ((bf16[16,64,128]{2,1,0:T(8,128)(2,1)}), bf16[16,64,128]{2,1,0:T(8,128)(2,1)S(1)}, u32[]{:S(2)}, u32[]{:S(2)}) async-start(bf16[16,64,128]{2,1,0:T(8,128)(2,1)} %copy-done.51), calls=%async_computation.2 | async-start | bytes 524288 | tf_op jit(solution)/shard_map/all_to_all | solution.py:160
  51.7 1.6 collective-permute-start.2
  53.2 8.4 %all-to-all-done.2.near = bf16[16,64,128]{2,1,0:T(8,128)(2,1)S(1)} async-done(((bf16[16,64,128]{2,1,0:T(8,128)(2,1)}), bf16[16,64,128]{2,1,0:T(8,128)(2,1)S(1)}, u32[]{:S(2)}, u32[]{:S(2)}) %all-to-all-start.2) | async-done | bytes 262176 | tf_op jit(solution)/shard_map/all_to_all | solution.py:160
  61.6 1.0 copy-done.8
  62.7 1.0 copy-done.14
  63.7 1.0 copy-done.16
  69.5 3.5 %all-to-all-start.3 = ((bf16[16,64,128]{2,1,0:T(8,128)(2,1)}), bf16[16,64,128]{2,1,0:T(8,128)(2,1)S(1)}, u32[]{:S(2)}, u32[]{:S(2)}) async-start(bf16[16,64,128]{2,1,0:T(8,128)(2,1)} %copy-done.49), calls=%async_computation.3 | async-start | bytes 524288 | tf_op jit(solution)/shard_map/all_to_all | solution.py:160
  73.1 1.6 collective-permute-start.3
  74.7 8.4 %all-to-all-done.3.near = bf16[16,64,128]{2,1,0:T(8,128)(2,1)S(1)} async-done(((bf16[16,64,128]{2,1,0:T(8,128)(2,1)}), bf16[16,64,128]{2,1,0:T(8,128)(2,1)S(1)}, u32[]{:S(2)}, u32[]{:S(2)}) %all-to-all-start.3) | async-done | bytes 262176 | tf_op jit(solution)/shard_map/all_to_all | solution.py:160
  83.1 1.0 copy-done.10
  84.1 1.0 copy-done.12
  85.1 0.9 copy-done.38
  89.1 3.5 %all-to-all-start.4 = ((bf16[16,64,128]{2,1,0:T(8,128)(2,1)}), bf16[16,64,128]{2,1,0:T(8,128)(2,1)S(1)}, u32[]{:S(2)}, u32[]{:S(2)}) async-start(bf16[16,64,128]{2,1,0:T(8,128)(2,1)} %copy-done.53), calls=%async_computation.4 | async-start | bytes 524288 | tf_op jit(solution)/shard_map/all_to_all | solution.py:160
  92.6 1.6 collective-permute-start.4
  94.2 8.4 %all-to-all-done.4.near = bf16[16,64,128]{2,1,0:T(8,128)(2,1)S(1)} async-done(((bf16[16,64,128]{2,1,0:T(8,128)(2,1)}), bf16[16,64,128]{2,1,0:T(8,128)(2,1)S(1)}, u32[]{:S(2)}, u32[]{:S(2)}) %all-to-all-start.4) | async-done | bytes 262176 | tf_op jit(solution)/shard_map/all_to_all | solution.py:160
  102.6 1.0 copy-done.2
  103.7 0.9 copy-done.40
  108.4 3.5 %all-to-all-start.5 = ((bf16[16,64,128]{2,1,0:T(8,128)(2,1)}), bf16[16,64,128]{2,1,0:T(8,128)(2,1)S(1)}, u32[]{:S(2)}, u32[]{:S(2)}) async-start(bf16[16,64,128]{2,1,0:T(8,128)(2,1)} %copy-done.55), calls=%async_computation.5 | async-start | bytes 524288 | tf_op jit(solution)/shard_map/all_to_all | solution.py:160
  111.9 1.6 collective-permute-start.5
  113.5 8.4 %all-to-all-done.5.near = bf16[16,64,128]{2,1,0:T(8,128)(2,1)S(1)} async-done(((bf16[16,64,128]{2,1,0:T(8,128)(2,1)}), bf16[16,64,128]{2,1,0:T(8,128)(2,1)S(1)}, u32[]{:S(2)}, u32[]{:S(2)}) %all-to-all-start.5) | async-done | bytes 262176 | tf_op jit(solution)/shard_map/all_to_all | solution.py:160
  121.9 1.0 copy-done.3
  123.0 1.0 copy-done.26
  124.0 1.0 copy-done.28
  129.8 3.5 %all-to-all-start.6 = ((bf16[16,64,128]{2,1,0:T(8,128)(2,1)}), bf16[16,64,128]{2,1,0:T(8,128)(2,1)S(1)}, u32[]{:S(2)}, u32[]{:S(2)}) async-start(bf16[16,64,128]{2,1,0:T(8,128)(2,1)} %copy-done.52), calls=%async_computation.6 | async-start | bytes 524288 | tf_op jit(solution)/shard_map/all_to_all | solution.py:160
  133.3 1.6 collective-permute-start.6
  134.9 8.4 %all-to-all-done.6.near = bf16[16,64,128]{2,1,0:T(8,128)(2,1)S(1)} async-done(((bf16[16,64,128]{2,1,0:T(8,128)(2,1)}), bf16[16,64,128]{2,1,0:T(8,128)(2,1)S(1)}, u32[]{:S(2)}, u32[]{:S(2)}) %all-to-all-start.6) | async-done | bytes 262176 | tf_op jit(solution)/shard_map/all_to_all | solution.py:160
  143.3 1.0 copy-done.4
  144.4 1.0 copy-done.18
  145.4 1.0 copy-done.20
  151.2 3.5 %all-to-all-start.7 = ((bf16[16,64,128]{2,1,0:T(8,128)(2,1)}), bf16[16,64,128]{2,1,0:T(8,128)(2,1)S(1)}, u32[]{:S(2)}, u32[]{:S(2)}) async-start(bf16[16,64,128]{2,1,0:T(8,128)(2,1)} %copy-done.50), calls=%async_computation.7 | async-start | bytes 524288 | tf_op jit(solution)/shard_map/all_to_all | solution.py:160
  154.8 1.6 collective-permute-start.7
  156.3 8.4 %all-to-all-done.7.near = bf16[16,64,128]{2,1,0:T(8,128)(2,1)S(1)} async-done(((bf16[16,64,128]{2,1,0:T(8,128)(2,1)}), bf16[16,64,128]{2,1,0:T(8,128)(2,1)S(1)}, u32[]{:S(2)}, u32[]{:S(2)}) %all-to-all-start.7) | async-done | bytes 262176 | tf_op jit(solution)/shard_map/all_to_all | solution.py:160
  164.7 1.0 copy-done.30
  165.8 1.0 copy-done.32
  167.8 1.5 stage.15
  (115 shorter events, 31.7 us)
Async XLA Ops:
  0.0 20.9 %copy-start = (bf16[16,6,128,128]{3,2,1,0:T(8,128)(2,1)S(1)}, bf16[16,6,128,128]{3,2,1,0:T(8,128)(2,1)}, u32[]{:S(2)}) copy-start(bf16[16,6,128,128]{3,2,1,0:T(8,128)(2,1)} %param.9) | copy-start | bytes 9437188
  1.3 0.8 copy-start.5
  3.5 17.4 %all-to-all-start = ((bf16[16,64,128]{2,1,0:T(8,128)(2,1)}), bf16[16,64,128]{2,1,0:T(8,128)(2,1)S(1)}, u32[]{:S(2)}, u32[]{:S(2)}) async-start(bf16[16,64,128]{2,1,0:T(8,128)(2,1)} %copy-done.56), calls=%async_computation | async-start | bytes 524288 | tf_op jit(solution)/shard_map/all_to_all | solution.py:160
  10.9 10.0 %collective-permute-start = (bf16[2,64,128]{2,1,0:T(8,128)(2,1)S(1)}, bf16[2,64,128]{2,1,0:T(8,128)(2,1)S(1)}, u32[]{:S(2)}, u32[]{:S(2)}) collective-permute-start(bf16[2,64,128]{2,1,0:T(8,128)(2,1)S(1)} %get-tuple-element.49), channel_id=1, source_target_pairs={{0,16},{16,0},{1,17},{17,1},{2,18},{18,2},{3,19},{19,3},{4,20},{20... | collective-permute-start | bytes 98312 | tf_op jit(solution)/shard_map/ppermute | solution.py:159
  20.9 1.0 copy-start.6
  22.0 0.9 copy-start.48
  24.5 0.8 copy-start.23
  26.7 13.5 %all-to-all-start.1 = ((bf16[16,64,128]{2,1,0:T(8,128)(2,1)}), bf16[16,64,128]{2,1,0:T(8,128)(2,1)S(1)}, u32[]{:S(2)}, u32[]{:S(2)}) async-start(bf16[16,64,128]{2,1,0:T(8,128)(2,1)} %copy-done.54), calls=%async_computation.1 | async-start | bytes 524288 | tf_op jit(solution)/shard_map/all_to_all | solution.py:160
  30.3 10.0 %collective-permute-start.1 = (bf16[2,64,128]{2,1,0:T(8,128)(2,1)S(1)}, bf16[2,64,128]{2,1,0:T(8,128)(2,1)S(1)}, u32[]{:S(2)}, u32[]{:S(2)}) collective-permute-start(bf16[2,64,128]{2,1,0:T(8,128)(2,1)S(1)} %get-tuple-element.53), channel_id=1, source_target_pairs={{0,16},{16,0},{1,17},{17,1},{2,18},{18,2},{3,19},{19,3},{4,20},{20... | collective-permute-start | bytes 98312 | tf_op jit(solution)/shard_map/ppermute | solution.py:159
  40.2 1.0 copy-start.7
  41.3 1.0 copy-start.22
  42.3 1.0 copy-start.24
  43.4 0.9 copy-start.42
  45.9 0.8 copy-start.15
  48.1 13.5 %all-to-all-start.2 = ((bf16[16,64,128]{2,1,0:T(8,128)(2,1)}), bf16[16,64,128]{2,1,0:T(8,128)(2,1)S(1)}, u32[]{:S(2)}, u32[]{:S(2)}) async-start(bf16[16,64,128]{2,1,0:T(8,128)(2,1)} %copy-done.51), calls=%async_computation.2 | async-start | bytes 524288 | tf_op jit(solution)/shard_map/all_to_all | solution.py:160
  51.7 10.0 %collective-permute-start.2 = (bf16[2,64,128]{2,1,0:T(8,128)(2,1)S(1)}, bf16[2,64,128]{2,1,0:T(8,128)(2,1)S(1)}, u32[]{:S(2)}, u32[]{:S(2)}) collective-permute-start(bf16[2,64,128]{2,1,0:T(8,128)(2,1)S(1)} %get-tuple-element.58), channel_id=1, source_target_pairs={{0,16},{16,0},{1,17},{17,1},{2,18},{18,2},{3,19},{19,3},{4,20},{20... | collective-permute-start | bytes 98312 | tf_op jit(solution)/shard_map/ppermute | solution.py:159
  61.6 1.0 copy-start.8
  62.7 1.0 copy-start.14
  63.7 1.0 copy-start.16
  64.8 0.9 copy-start.34
  69.5 13.5 %all-to-all-start.3 = ((bf16[16,64,128]{2,1,0:T(8,128)(2,1)}), bf16[16,64,128]{2,1,0:T(8,128)(2,1)S(1)}, u32[]{:S(2)}, u32[]{:S(2)}) async-start(bf16[16,64,128]{2,1,0:T(8,128)(2,1)} %copy-done.49), calls=%async_computation.3 | async-start | bytes 524288 | tf_op jit(solution)/shard_map/all_to_all | solution.py:160
  73.1 10.0 %collective-permute-start.3 = (bf16[2,64,128]{2,1,0:T(8,128)(2,1)S(1)}, bf16[2,64,128]{2,1,0:T(8,128)(2,1)S(1)}, u32[]{:S(2)}, u32[]{:S(2)}) collective-permute-start(bf16[2,64,128]{2,1,0:T(8,128)(2,1)S(1)} %get-tuple-element.63), channel_id=1, source_target_pairs={{0,16},{16,0},{1,17},{17,1},{2,18},{18,2},{3,19},{19,3},{4,20},{20... | collective-permute-start | bytes 98312 | tf_op jit(solution)/shard_map/ppermute | solution.py:159
  83.1 1.0 copy-start.10
  84.1 1.0 copy-start.12
  85.1 0.9 copy-start.38
  89.1 13.5 %all-to-all-start.4 = ((bf16[16,64,128]{2,1,0:T(8,128)(2,1)}), bf16[16,64,128]{2,1,0:T(8,128)(2,1)S(1)}, u32[]{:S(2)}, u32[]{:S(2)}) async-start(bf16[16,64,128]{2,1,0:T(8,128)(2,1)} %copy-done.53), calls=%async_computation.4 | async-start | bytes 524288 | tf_op jit(solution)/shard_map/all_to_all | solution.py:160
  92.6 10.0 %collective-permute-start.4 = (bf16[2,64,128]{2,1,0:T(8,128)(2,1)S(1)}, bf16[2,64,128]{2,1,0:T(8,128)(2,1)S(1)}, u32[]{:S(2)}, u32[]{:S(2)}) collective-permute-start(bf16[2,64,128]{2,1,0:T(8,128)(2,1)S(1)} %get-tuple-element.68), channel_id=1, source_target_pairs={{0,16},{16,0},{1,17},{17,1},{2,18},{18,2},{3,19},{19,3},{4,20},{20... | collective-permute-start | bytes 98312 | tf_op jit(solution)/shard_map/ppermute | solution.py:159
  102.6 1.0 copy-start.2
  103.6 0.9 copy-start.40
  106.2 0.8 copy-start.27
  108.4 13.5 %all-to-all-start.5 = ((bf16[16,64,128]{2,1,0:T(8,128)(2,1)}), bf16[16,64,128]{2,1,0:T(8,128)(2,1)S(1)}, u32[]{:S(2)}, u32[]{:S(2)}) async-start(bf16[16,64,128]{2,1,0:T(8,128)(2,1)} %copy-done.55), calls=%async_computation.5 | async-start | bytes 524288 | tf_op jit(solution)/shard_map/all_to_all | solution.py:160
  111.9 10.0 %collective-permute-start.5 = (bf16[2,64,128]{2,1,0:T(8,128)(2,1)S(1)}, bf16[2,64,128]{2,1,0:T(8,128)(2,1)S(1)}, u32[]{:S(2)}, u32[]{:S(2)}) collective-permute-start(bf16[2,64,128]{2,1,0:T(8,128)(2,1)S(1)} %get-tuple-element.72), channel_id=1, source_target_pairs={{0,16},{16,0},{1,17},{17,1},{2,18},{18,2},{3,19},{19,3},{4,20},{20... | collective-permute-start | bytes 98312 | tf_op jit(solution)/shard_map/ppermute | solution.py:159
  121.9 1.0 copy-start.3
  123.0 1.0 copy-start.26
  124.0 1.0 copy-start.28
  125.1 0.9 copy-start.44
  127.6 0.8 copy-start.19
  129.8 13.5 %all-to-all-start.6 = ((bf16[16,64,128]{2,1,0:T(8,128)(2,1)}), bf16[16,64,128]{2,1,0:T(8,128)(2,1)S(1)}, u32[]{:S(2)}, u32[]{:S(2)}) async-start(bf16[16,64,128]{2,1,0:T(8,128)(2,1)} %copy-done.52), calls=%async_computation.6 | async-start | bytes 524288 | tf_op jit(solution)/shard_map/all_to_all | solution.py:160
  133.3 10.0 %collective-permute-start.6 = (bf16[2,64,128]{2,1,0:T(8,128)(2,1)S(1)}, bf16[2,64,128]{2,1,0:T(8,128)(2,1)S(1)}, u32[]{:S(2)}, u32[]{:S(2)}) collective-permute-start(bf16[2,64,128]{2,1,0:T(8,128)(2,1)S(1)} %get-tuple-element.77), channel_id=1, source_target_pairs={{0,16},{16,0},{1,17},{17,1},{2,18},{18,2},{3,19},{19,3},{4,20},{20... | collective-permute-start | bytes 98312 | tf_op jit(solution)/shard_map/ppermute | solution.py:159
  143.3 1.0 copy-start.4
  144.4 1.0 copy-start.18
  145.4 1.0 copy-start.20
  146.5 0.9 copy-start.36
  151.2 13.5 %all-to-all-start.7 = ((bf16[16,64,128]{2,1,0:T(8,128)(2,1)}), bf16[16,64,128]{2,1,0:T(8,128)(2,1)S(1)}, u32[]{:S(2)}, u32[]{:S(2)}) async-start(bf16[16,64,128]{2,1,0:T(8,128)(2,1)} %copy-done.50), calls=%async_computation.7 | async-start | bytes 524288 | tf_op jit(solution)/shard_map/all_to_all | solution.py:160
  154.8 10.0 %collective-permute-start.7 = (bf16[2,64,128]{2,1,0:T(8,128)(2,1)S(1)}, bf16[2,64,128]{2,1,0:T(8,128)(2,1)S(1)}, u32[]{:S(2)}, u32[]{:S(2)}) collective-permute-start(bf16[2,64,128]{2,1,0:T(8,128)(2,1)S(1)} %get-tuple-element.82), channel_id=1, source_target_pairs={{0,16},{16,0},{1,17},{17,1},{2,18},{18,2},{3,19},{19,3},{4,20},{20... | collective-permute-start | bytes 98312 | tf_op jit(solution)/shard_map/ppermute | solution.py:159
  164.7 1.0 copy-start.30
  165.8 1.0 copy-start.32
  166.8 0.9 copy-start.46
  (25 other events, 18.4 us)
